TPU v7x, 8 devices: a whole 2x2x1 slice. The times are simulated.
8 devices in a mesh: dp: 1 (over z), sp: 8 (over y, x, core).
Axes of the slice: x: 2, y: 2, z: 1, core: 2. Of those that a mesh axis runs over, the one named last changes fastest.
Arguments:
- hidden: bfloat16 [49152, 2048], P(('dp', 'sp'))
- tok_perm: int32 [49152], P(('dp', 'sp'))
- send_off: int32 [64], P(('dp', 'sp'))
- send_len: int32 [64], P(('dp', 'sp'))
- recv_off: int32 [64], P(('dp', 'sp'))
- recv_len: int32 [64], P(('dp', 'sp'))
- recv_doc: int32 [24576], P(('dp', 'sp'))
- recv_pos: int32 [24576], P(('dp', 'sp'))
- g_attn: bfloat16 [2048], replicated
- w_q: bfloat16 [2048, 16, 128], replicated
- w_k: bfloat16 [2048, 2, 128], replicated
- w_v: bfloat16 [2048, 2, 128], replicated
- w_o: bfloat16 [16, 128, 2048], replicated
- g_mlp: bfloat16 [2048], replicated
- w_gate: bfloat16 [2048, 11008], replicated
- w_up: bfloat16 [2048, 11008], replicated
- w_down: bfloat16 [11008, 2048], replicated
Outputs:
- output: bfloat16 [49152, 2048], P(('dp', 'sp'))
All inputs are finite; a program needn't handle non-finite values.
Results may differ from a plain program's by a relative error of at most 0.0108789.
Values are sent between devices in bfloat16 or wider.
A program may use at most 1 GiB of HBM per device.

v0:
```python
import jax
import jax.numpy as jnp
from jax import lax
from jax.sharding import PartitionSpec as P

Q_BLOCK = 128
ROPE_BASE = 500000.0
NORM_EPS = 1e-5


def rms_norm(rows_in, gain_vec):
    rows_f = rows_in.astype(jnp.float32)
    inv_rms = lax.rsqrt(jnp.mean(rows_f * rows_f, axis=-1, keepdims=True) + NORM_EPS)
    return (rows_f * inv_rms * gain_vec.astype(jnp.float32)).astype(jnp.bfloat16)


def rope(proj, positions):
    head_dim = proj.shape[-1]
    half_dim = head_dim // 2
    inv_freq = jnp.power(jnp.float32(ROPE_BASE), -2.0 * jnp.arange(half_dim, dtype=jnp.float32) / head_dim)
    angles = positions.astype(jnp.float32)[:, None, None] * inv_freq[None, None, :]
    cos_t = jnp.cos(angles)
    sin_t = jnp.sin(angles)
    lo_half = proj[..., :half_dim]
    hi_half = proj[..., half_dim:]
    return jnp.concatenate([lo_half * cos_t - hi_half * sin_t, hi_half * cos_t + lo_half * sin_t], axis=-1)


def attend(q_rot, k_rot, v_proj, doc_ids, positions):
    n_rows, n_kv, q_per_kv, head_dim = q_rot.shape
    n_blocks = n_rows // Q_BLOCK
    qk_scale = head_dim ** -0.5

    def one_block(blk_args):
        q_blk, doc_q, pos_q = blk_args
        scores = jnp.einsum('qkgd,skd->kgqs', q_blk, k_rot, preferred_element_type=jnp.float32) * qk_scale
        allowed = (doc_q[:, None] == doc_ids[None, :]) & (positions[None, :] <= pos_q[:, None])
        probs_bf = jax.nn.softmax(jnp.where(allowed, scores, -1e30), axis=-1).astype(jnp.bfloat16)
        return jnp.einsum('kgqs,skd->qkgd', probs_bf, v_proj, preferred_element_type=jnp.float32).astype(jnp.bfloat16)

    blocks_out = lax.map(one_block, (q_rot.reshape(n_blocks, Q_BLOCK, n_kv, q_per_kv, head_dim), doc_ids.reshape(n_blocks, Q_BLOCK), positions.reshape(n_blocks, Q_BLOCK)))
    return blocks_out.reshape(n_rows, n_kv, q_per_kv, head_dim)


def layer(dest_rows, doc_ids, positions, g_attn, w_q, w_k, w_v, w_o, g_mlp, w_gate, w_up, w_down):
    n_rows, model_dim = dest_rows.shape
    n_heads = w_q.shape[1]
    head_dim = w_q.shape[2]
    n_kv = w_k.shape[1]
    normed = rms_norm(dest_rows, g_attn)
    q_proj = jnp.einsum('td,dhe->the', normed, w_q, preferred_element_type=jnp.float32)
    k_proj = jnp.einsum('td,dhe->the', normed, w_k, preferred_element_type=jnp.float32)
    v_proj = jnp.einsum('td,dhe->the', normed, w_v, preferred_element_type=jnp.float32).astype(jnp.bfloat16)
    q_rot = rope(q_proj, positions).astype(jnp.bfloat16).reshape(n_rows, n_kv, n_heads // n_kv, head_dim)
    k_rot = rope(k_proj, positions).astype(jnp.bfloat16)
    attn_heads = attend(q_rot, k_rot, v_proj, doc_ids, positions)
    attn_out = jnp.einsum('qkgd,kgde->qe', attn_heads, w_o.reshape(n_kv, n_heads // n_kv, head_dim, model_dim), preferred_element_type=jnp.float32).astype(jnp.bfloat16)
    resid_mid = (dest_rows.astype(jnp.float32) + attn_out.astype(jnp.float32)).astype(jnp.bfloat16)
    normed_mlp = rms_norm(resid_mid, g_mlp)
    gate_proj = jnp.dot(normed_mlp, w_gate, preferred_element_type=jnp.float32)
    up_proj = jnp.dot(normed_mlp, w_up, preferred_element_type=jnp.float32)
    hidden_act = (jax.nn.silu(gate_proj) * up_proj).astype(jnp.bfloat16)
    down_proj = jnp.dot(hidden_act, w_down, preferred_element_type=jnp.float32).astype(jnp.bfloat16)
    return (resid_mid.astype(jnp.float32) + down_proj.astype(jnp.float32)).astype(jnp.bfloat16)


def solution(mesh):
    row_spec = P(('dp', 'sp'), None)
    vec_spec = P(('dp', 'sp'))
    rep_spec = P()

    def per_device(hidden, tok_perm, send_off, send_len, recv_off, recv_len, recv_doc, recv_pos, g_attn, w_q, w_k, w_v, w_o, g_mlp, w_gate, w_up, w_down):
        n_tok, model_dim = hidden.shape
        n_cap = recv_doc.shape[0]
        group_devs = send_off.shape[0]
        zero_val = jnp.zeros((), hidden.dtype)
        pair_row = jnp.arange(n_cap)[None, :]
        dev_base = jnp.arange(group_devs)[None, :] * n_cap
        send_idx = jnp.minimum(send_off[:, None] + pair_row, n_tok - 1).reshape(-1)
        send_buf = jnp.take(hidden, jnp.take(tok_perm, send_idx), axis=0).reshape(group_devs, n_cap, model_dim)
        recv_buf = lax.all_to_all(send_buf, 'sp', 0, 0, tiled=True).reshape(group_devs * n_cap, model_dim)
        slot_idx = jnp.arange(n_cap)[:, None]
        in_run = (slot_idx >= recv_off[None, :]) & (slot_idx < (recv_off + recv_len)[None, :])
        flat_pos = jnp.sum(jnp.where(in_run, dev_base + slot_idx - recv_off[None, :], 0), axis=1)
        dest_rows = jnp.take(recv_buf, flat_pos, axis=0)
        layer_rows = layer(dest_rows, recv_doc, recv_pos, g_attn, w_q, w_k, w_v, w_o, g_mlp, w_gate, w_up, w_down)
        back_idx = jnp.minimum(recv_off[:, None] + pair_row, n_cap - 1).reshape(-1)
        back_buf = jnp.take(layer_rows, back_idx, axis=0).reshape(group_devs, n_cap, model_dim)
        back_recv = lax.all_to_all(back_buf, 'sp', 0, 0, tiled=True).reshape(group_devs * n_cap, model_dim)
        inv_perm = jnp.argsort(tok_perm)[:, None]
        in_back = (inv_perm >= send_off[None, :]) & (inv_perm < (send_off + send_len)[None, :])
        back_pos = jnp.sum(jnp.where(in_back, dev_base + inv_perm - send_off[None, :], 0), axis=1)
        was_sent = jnp.any(in_back, axis=1)
        return jnp.where(was_sent[:, None], jnp.take(back_recv, back_pos, axis=0), zero_val)

    return jax.shard_map(per_device, mesh=mesh, in_specs=(row_spec,) + (vec_spec,) * 7 + (rep_spec,) * 9, out_specs=row_spec, check_vma=False)
```

profile of v0, /device:TPU:3, one launch (start us, length us, event | category | flops | bytes accessed | tf_op | source)
XLA Modules:
  0.0 4582.7 jit_solution(16067290458440080861)
XLA Ops:
  1.1 135.5 %gather_fusion = s32[24576]{0:T(1024)S(1)} fusion(s32[6144]{0:T(1024)S(1)} %copy-done.2, s32[24576]{0:T(1024)S(1)} %broadcast_clamp_fusion.2), kind=kCustom, calls=%fused_computation | custom fusion | bytes 294912 | tf_op jit(solution)/shard_map/jit(_take)/gather | solution.py:80
  137.7 192.8 %gather_fusion.1 = bf16[24576,2048]{1,0:T(8,128)(2,1)} fusion(bf16[6144,2048]{1,0:T(8,128)(2,1)} %param.19, s32[24576]{0:T(1024)S(1)} %broadcast_clamp_fusion.1), kind=kCustom, calls=%fused_computation.1 | custom fusion | bytes 201424896 | tf_op jit(solution)/shard_map/jit(_take)/gather | solution.py:80
  330.5 65.3 %broadcast_select_fusion = bf16[8,3072,2048]{2,1,0:T(8,128)(2,1)} fusion(bf16[8,3072,2048]{2,1,0:T(8,128)(2,1)} %bitcast.13, pred[8,3072]{1,0:T(8,128)(4,1)S(1)} %copy-done.13), kind=kLoop, calls=%fused_computation.38 | loop fusion | flops 50331648 | bytes 201351168 | tf_op jit(solution)/shard_map/jit(_take)/select_n | solution.py:80
  395.9 10.8 all-to-all-start
  408.9 12.4 copy.48
  427.0 1060.4 %all-to-all-done = bf16[8,3072,2048]{2,1,0:T(8,128)(2,1)} async-done(((bf16[8,3072,2048]{2,1,0:T(8,128)(2,1)}), bf16[8,3072,2048]{2,1,0:T(8,128)(2,1)}, u32[]{:S(2)}, u32[]{:S(2)}) %all-to-all-start) | async-done | bytes 100663328 | tf_op jit(solution)/shard_map/all_to_all | solution.py:81
  1487.4 71.6 %gather_fusion.2 = bf16[3072,2048]{1,0:T(8,128)(2,1)} fusion(bf16[24576,2048]{1,0:T(8,128)(2,1)} %bitcast.14, s32[3072]{0:T(1024)S(1)} %broadcast_clamp_fusion.4), kind=kCustom, calls=%fused_computation.2 | custom fusion | bytes 25178112 | tf_op jit(solution)/shard_map/jit(_take)/gather | solution.py:85
  1559.0 16.6 copy.46
  1595.5 34.8 fusion.73
  1630.3 12.8 subtract_convert_fusion
  1647.8 12.6 copy.49
  1667.7 12.8 copy.50
  1680.6 10.9 fusion.55
  1691.5 14.0 pad_maximum_fusion
  1705.5 649.4 %while.10 = (s32[]{:T(128)}, bf16[24,128,2,8,128]{4,3,2,1,0:T(8,128)(2,1)}, s32[24,128]{1,0:T(8,128)S(1)}, s32[3072]{0:T(1024)S(1)}, s32[3072]{0:T(1024)S(1)}, /...) while((s32[]{:T(128)}, ...), condition=%wide.region_8.9_spmd, body=%wide.region_5.8_spmd.sunk | while | flops 3260419072 | bytes 56406120 | solution.py:41
  1706.1 15.0 fusion.108
  1721.0 10.5 fusion.109
  1733.1 15.0 fusion.108
  1748.1 10.5 fusion.109
  1760.2 15.0 fusion.108
  1775.1 10.5 fusion.109
  1787.2 15.0 fusion.108
  1802.2 10.5 fusion.109
  1814.3 15.0 fusion.108
  1829.2 10.5 fusion.109
  1841.3 15.0 fusion.108
  1856.3 10.5 fusion.109
  1868.4 15.0 fusion.108
  1883.3 10.5 fusion.109
  1895.4 15.0 fusion.108
  1910.4 10.5 fusion.109
  1922.5 15.0 fusion.108
  1937.4 10.5 fusion.109
  1949.5 15.0 fusion.108
  1964.4 10.5 fusion.109
  1976.5 15.0 fusion.108
  1991.5 10.5 fusion.109
  2003.6 15.0 fusion.108
  2018.5 10.5 fusion.109
  2030.6 15.0 fusion.108
  2045.6 10.5 fusion.109
  2057.7 15.0 fusion.108
  2072.6 10.5 fusion.109
  2084.7 15.0 fusion.108
  2111.8 15.0 fusion.108
  2138.8 15.0 fusion.108
  2165.9 15.0 fusion.108
  2193.0 15.0 fusion.108
  2220.0 15.0 fusion.108
  2247.1 15.0 fusion.108
  2274.1 15.0 fusion.108
  2301.1 15.0 fusion.108
  2328.2 15.0 fusion.108
  2354.9 38.6 fusion.45
  2393.5 160.8 %fusion.59 = f32[3072,11008]{1,0:T(8,128)} fusion(bf16[2048,11008]{1,0:T(8,128)(2,1)} %param.33, bf16[3072,2048]{0,1:T(8,128)(2,1)} %get-tuple-element.111, f32[2048]{0:T(1024)S(1)} %copy-done.18, f32[3072]{0:T(1024)S(1)} %add_rsqrt_fusion), kind=kOutput, calls=%fused_computation.65 | convolution fusion | flops 138537861120 | bytes 192958464 | tf_op jit(solution)/shard_map/dot_general | solution.py:60
  2554.2 193.1 %multiply_convert_fusion = bf16[3072,11008]{1,0:T(8,128)(2,1)} fusion(f32[3072,11008]{1,0:T(8,128)} %fusion.59, bf16[2048,11008]{1,0:T(8,128)(2,1)} %param.34, bf16[3072,2048]{0,1:T(8,128)(2,1)} %get-tuple-element.111, f32[2048]{0:T(1024)S(1)} %copy-done.18, f32[3072]{0:T(1024)S(1)} %add_rsqrt_fusion), kind=kOutput, calls=%fused_computation.37 | convolution fusion | flops 138740760576 | bytes 260591616 | tf_op jit(solution)/shard_map/dot_general | solution.py:61
  2747.3 159.1 %fusion.48 = bf16[3072,2048]{0,1:T(8,128)(2,1)} fusion(bf16[3072,2048]{0,1:T(8,128)(2,1)} %get-tuple-element.111, bf16[3072,11008]{1,0:T(8,128)(2,1)} %multiply_convert_fusion, bf16[11008,2048]{1,0:T(8,128)(2,1)} %param.35), kind=kOutput, calls=%fused_computation.53 | convolution fusion | flops 138544152576 | bytes 137887744 | tf_op jit(solution)/shard_map/dot_general | solution.py:63
  2906.4 16.8 copy.60
  2923.2 187.6 %gather_fusion.3 = bf16[24576,2048]{1,0:T(8,128)(2,1)} fusion(bf16[3072,2048]{1,0:T(8,128)(2,1)} %copy.60, s32[24576]{0:T(1024)S(1)} %copy-done.10), kind=kCustom, calls=%fused_computation.3 | custom fusion | bytes 201424896 | tf_op jit(solution)/shard_map/jit(_take)/gather | solution.py:88
  3110.8 64.9 %broadcast_select_fusion.1 = bf16[8,3072,2048]{2,1,0:T(8,128)(2,1)} fusion(bf16[8,3072,2048]{2,1,0:T(8,128)(2,1)} %bitcast.29, pred[8,3072]{1,0:T(8,128)(4,1)S(1)} %copy-done.12), kind=kLoop, calls=%fused_computation.39 | loop fusion | flops 50331648 | bytes 201351168 | tf_op jit(solution)/shard_map/jit(_take)/select_n | solution.py:88
  3175.7 14.1 all-to-all-start.1
  3197.0 1073.5 %all-to-all-done.1 = bf16[8,3072,2048]{2,1,0:T(8,128)(2,1)} async-done(((bf16[8,3072,2048]{2,1,0:T(8,128)(2,1)}), bf16[8,3072,2048]{2,1,0:T(8,128)(2,1)}, u32[]{:S(2)}, u32[]{:S(2)}) %all-to-all-start.1) | async-done | bytes 100663328 | tf_op jit(solution)/shard_map/all_to_all | solution.py:89
  4270.5 289.6 %gather_fusion.4 = bf16[6144,2048]{1,0:T(8,128)(2,1)} fusion(bf16[24576,2048]{1,0:T(8,128)(2,1)} %bitcast.30, s32[6144]{0:T(1024)S(1)} %broadcast_clamp_fusion.3), kind=kCustom, calls=%fused_computation.4 | custom fusion | bytes 50356224 | tf_op jit(solution)/shard_map/jit(_take)/gather | solution.py:94
  4560.1 22.4 select_select_fusion
  (177 shorter events, 190.9 us)
Async XLA Ops:
  0.0 1680.5 %copy-start = (bf16[2048,2,128]{2,1,0:T(2,128)(2,1)S(1)}, bf16[2048,2,128]{2,1,0:T(2,128)(2,1)}, u32[]{:S(2)}) copy-start(bf16[2048,2,128]{2,1,0:T(2,128)(2,1)} %param.30) | copy-start | bytes 3145732
  0.0 1.1 copy-start.2
  1.1 135.9 %copy-start.16 = (s32[8]{0:T(128)S(1)}, s32[8]{0:T(128)}, u32[]{:S(2)}) copy-start(s32[8]{0:T(128)} %param.21) | copy-start | bytes 100
  137.7 192.8 %copy-start.13 = (pred[8,3072]{1,0:T(8,128)(4,1)S(1)}, pred[8,3072]{1,0:T(8,128)(4,1)}, u32[]{:S(2)}) copy-start(pred[8,3072]{1,0:T(8,128)(4,1)} %compare_and_fusion.2) | copy-start | bytes 73732
  395.9 10.9 copy-start.20
  395.9 10.9 copy-start.6
  395.9 13.0 copy-start.8
  395.9 1091.5 %all-to-all-start = ((bf16[8,3072,2048]{2,1,0:T(8,128)(2,1)}), bf16[8,3072,2048]{2,1,0:T(8,128)(2,1)}, u32[]{:S(2)}, u32[]{:S(2)}) async-start(bf16[8,3072,2048]{2,1,0:T(8,128)(2,1)} %broadcast_select_fusion), calls=%async_computation | async-start | bytes 201326592 | tf_op jit(solution)/shard_map/all_to_all | solution.py:81
  406.8 14.6 copy-start.21
  406.8 15.2 copy-start.19
  406.8 15.2 copy-start.24
  422.2 0.5 copy-start.22
  422.3 1258.2 %copy-start.14 = (pred[3072]{0:T(1024)(128)(4,1)}, pred[3072]{0:T(1024)(128)(4,1)S(1)}, u32[]{:S(2)}) copy-start(pred[3072]{0:T(1024)(128)(4,1)S(1)} %compare_and_fusion.4) | copy-start | bytes 9220
  1575.7 8.0 copy-start.7
  1680.5 10.9 copy-start.4
  1691.5 14.0 copy-start.5
  1691.5 14.0 copy-start.9
  1691.5 14.0 copy-start.11
  1705.5 649.4 %copy-start.15 = (pred[3072]{0:T(1024)(128)(4,1)S(1)}, pred[3072]{0:T(1024)(128)(4,1)}, u32[]{:S(2)}) copy-start(pred[3072]{0:T(1024)(128)(4,1)} %copy-done.14) | copy-start | bytes 9220
  2354.9 38.6 copy-start.18
  2906.4 16.8 copy-start.10
  2923.2 187.6 %copy-start.12 = (pred[8,3072]{1,0:T(8,128)(4,1)S(1)}, pred[8,3072]{1,0:T(8,128)(4,1)}, u32[]{:S(2)}) copy-start(pred[8,3072]{1,0:T(8,128)(4,1)} %fusion.69) | copy-start | bytes 73732
  3175.7 14.2 copy-start.3
  3175.7 20.9 copy-start.17
  3175.7 20.9 copy-start.25
  3175.7 21.1 copy-start.23
  3175.7 1094.8 %all-to-all-start.1 = ((bf16[8,3072,2048]{2,1,0:T(8,128)(2,1)}), bf16[8,3072,2048]{2,1,0:T(8,128)(2,1)}, u32[]{:S(2)}, u32[]{:S(2)}) async-start(bf16[8,3072,2048]{2,1,0:T(8,128)(2,1)} %broadcast_select_fusion.1), calls=%async_computation.1 | async-start | bytes 201326592 | tf_op jit(solution)/shard_map/all_to_all | solution.py:89
  4560.1 22.4 copy-start.1
where the time goes:
time: 4600 us; the launch traced here: 4580 us
  waiting for transfers between devices  2130 us (46%)
  matrix products  1220 us (27%)
  local copies, waits for them, and re-layouts  994 us (22%)
  other arithmetic  212 us (5%)
    all_to_all x1, waiting for transfers between devices, per_device(): lax.all_to_all(back_buf, 'sp', 0, 0, tiled=True)  1070 us
    all_to_all x1, waiting for transfers between devices, per_device(): lax.all_to_all(send_buf, 'sp', 0, 0, tiled=True)  1060 us
    sub x24, matrix products, one_block(): jax.nn.softmax(jnp.where(allowed, scores, -1e+30), axis=-1)  359 us
    gather x1, local copies, waits for them, and re-layouts, per_device(): jnp.take(back_recv, back_pos, axis=0)  290 us
    dot_general x24, matrix products, one_block(): jnp.einsum('kgqs,skd->qkgd', probs_bf, v_proj, preferred_element_type=jnp...  253 us
    dot_general x1, matrix products, layer(): up_proj = jnp.dot(normed_mlp, w_up, preferred_element_type=jnp.float32)  193 us
    gather x1, local copies, waits for them, and re-layouts, per_device(): jnp.take(hidden, jnp.take(tok_perm, send_idx), axis=0)  193 us
    gather x1, local copies, waits for them, and re-layouts, per_device(): jnp.take(layer_rows, back_idx, axis=0).reshape(group_devs, n_cap, model_dim)  188 us
  transfers between devices with their start and end apart: 2, of which 2 were waited for; matrix products, arithmetic and copies ran while one was open for 1% of the time, Pallas kernels for 0%

commit v1 on v0

v1 whole, which is shorter than its diff:
```python
import functools

import jax
import jax.numpy as jnp
from jax import lax
from jax.experimental import pallas as pl
from jax.experimental.layout import Layout, with_layout_constraint
from jax.experimental.pallas import tpu as pltpu
from jax.sharding import PartitionSpec as P

Q_BLOCK = 128
ROPE_BASE = 500000.0
NORM_EPS = 1e-5
NEG = -1e30
LOG2E = 1.4426950408889634

BQ = 512
BK = 512
HEAD_ROWS = 1024
LEVELS = (1024, 1536, 2048, 3072)


def row_major(x):
    return with_layout_constraint(x, Layout(major_to_minor=tuple(range(x.ndim))))


def rms_norm(rows_in, gain_vec):
    rows_f = rows_in.astype(jnp.float32)
    inv_rms = lax.rsqrt(jnp.mean(rows_f * rows_f, axis=-1, keepdims=True) + NORM_EPS)
    return (rows_f * inv_rms * gain_vec.astype(jnp.float32)).astype(jnp.bfloat16)


def rope_tables(positions, head_dim):
    half_dim = head_dim // 2
    inv_freq = jnp.power(jnp.float32(ROPE_BASE), -2.0 * jnp.arange(half_dim, dtype=jnp.float32) / head_dim)
    angles = positions.astype(jnp.float32)[:, None] * inv_freq[None, :]
    return jnp.cos(angles), jnp.sin(angles)


def rope(proj, tables):
    cos_t, sin_t = tables[0][:, None, :], tables[1][:, None, :]
    half_dim = proj.shape[-1] // 2
    lo_half = proj[..., :half_dim]
    hi_half = proj[..., half_dim:]
    return jnp.concatenate([lo_half * cos_t - hi_half * sin_t, hi_half * cos_t + lo_half * sin_t], axis=-1)


def attend_general(q_rot, k_rot, v_proj, doc_ids, positions):
    n_rows, n_kv, q_per_kv, head_dim = q_rot.shape
    n_blocks = n_rows // Q_BLOCK
    qk_scale = head_dim ** -0.5

    def one_block(blk_args):
        q_blk, doc_q, pos_q = blk_args
        scores = jnp.einsum('qkgd,skd->kgqs', q_blk, k_rot, preferred_element_type=jnp.float32) * qk_scale
        allowed = (doc_q[:, None] == doc_ids[None, :]) & (positions[None, :] <= pos_q[:, None])
        probs_bf = jax.nn.softmax(jnp.where(allowed, scores, NEG), axis=-1).astype(jnp.bfloat16)
        return jnp.einsum('kgqs,skd->qkgd', probs_bf, v_proj, preferred_element_type=jnp.float32).astype(jnp.bfloat16)

    blocks_out = lax.map(one_block, (q_rot.reshape(n_blocks, Q_BLOCK, n_kv, q_per_kv, head_dim), doc_ids.reshape(n_blocks, Q_BLOCK), positions.reshape(n_blocks, Q_BLOCK)))
    return blocks_out.reshape(n_rows, n_kv * q_per_kv * head_dim)


def qkv(rows, positions, g_attn, w_q, w_k, w_v):
    normed = rms_norm(rows, g_attn)
    tables = lax.optimization_barrier(rope_tables(positions, w_q.shape[2]))
    k_proj = jnp.einsum('td,dhe->the', normed, w_k, preferred_element_type=jnp.float32)
    v_proj = jnp.einsum('td,dhe->the', normed, w_v, preferred_element_type=jnp.float32).astype(jnp.bfloat16)
    q_proj = jnp.einsum('td,dhe->the', normed, w_q, preferred_element_type=jnp.float32)
    return rope(q_proj, tables).astype(jnp.bfloat16), rope(k_proj, tables).astype(jnp.bfloat16), v_proj


def attn_residual(rows, attn_heads, w_o):
    attn_out = jnp.dot(attn_heads, w_o.reshape(-1, rows.shape[1]), preferred_element_type=jnp.float32).astype(jnp.bfloat16)
    return (rows.astype(jnp.float32) + attn_out.astype(jnp.float32)).astype(jnp.bfloat16)


def mlp_residual(resid_mid, g_mlp, w_gate, w_up, w_down):
    normed_mlp = rms_norm(resid_mid, g_mlp)
    gate_proj = jnp.dot(normed_mlp, w_gate, preferred_element_type=jnp.float32)
    up_proj = jnp.dot(normed_mlp, w_up, preferred_element_type=jnp.float32)
    hidden_act = (jax.nn.silu(gate_proj) * up_proj).astype(jnp.bfloat16)
    down_proj = jnp.dot(hidden_act, w_down, preferred_element_type=jnp.float32).astype(jnp.bfloat16)
    return (resid_mid.astype(jnp.float32) + down_proj.astype(jnp.float32)).astype(jnp.bfloat16)


def general_path(hidden, tok_perm, send_off, send_len, recv_off, recv_len, recv_doc, recv_pos, g_attn, w_q, w_k, w_v, w_o, g_mlp, w_gate, w_up, w_down):
    n_tok, model_dim = hidden.shape
    n_cap = recv_doc.shape[0]
    group_devs = send_off.shape[0]
    zero_val = jnp.zeros((), hidden.dtype)
    pair_row = jnp.arange(n_cap)[None, :]
    dev_base = jnp.arange(group_devs)[None, :] * n_cap
    send_idx = jnp.minimum(send_off[:, None] + pair_row, n_tok - 1).reshape(-1)
    send_buf = jnp.take(hidden, jnp.take(tok_perm, send_idx), axis=0).reshape(group_devs, n_cap, model_dim)
    recv_buf = lax.all_to_all(send_buf, 'sp', 0, 0, tiled=True).reshape(group_devs * n_cap, model_dim)
    slot_idx = jnp.arange(n_cap)[:, None]
    in_run = (slot_idx >= recv_off[None, :]) & (slot_idx < (recv_off + recv_len)[None, :])
    flat_pos = jnp.sum(jnp.where(in_run, dev_base + slot_idx - recv_off[None, :], 0), axis=1)
    rows = jnp.take(recv_buf, flat_pos, axis=0)
    q_rot, k_rot, v_proj = qkv(rows, recv_pos, g_attn, w_q, w_k, w_v)
    n_kv = w_k.shape[1]
    heads = attend_general(q_rot.reshape(n_cap, n_kv, -1, w_q.shape[2]), k_rot, v_proj, recv_doc, recv_pos)
    layer_rows = mlp_residual(attn_residual(rows, heads, w_o), g_mlp, w_gate, w_up, w_down)
    back_idx = jnp.minimum(recv_off[:, None] + pair_row, n_cap - 1).reshape(-1)
    back_buf = jnp.take(layer_rows, back_idx, axis=0).reshape(group_devs, n_cap, model_dim)
    back_recv = lax.all_to_all(back_buf, 'sp', 0, 0, tiled=True).reshape(group_devs * n_cap, model_dim)
    inv_perm = jnp.argsort(tok_perm)[:, None]
    in_back = (inv_perm >= send_off[None, :]) & (inv_perm < (send_off + send_len)[None, :])
    back_pos = jnp.sum(jnp.where(in_back, dev_base + inv_perm - send_off[None, :], 0), axis=1)
    was_sent = jnp.any(in_back, axis=1)
    return jnp.where(was_sent[:, None], jnp.take(back_recv, back_pos, axis=0), zero_val)


def flash_kernel(lomin_ref, lomax_ref, lo_ref, q_ref, k_ref, v_ref, o_ref, m_ref, l_ref, acc_ref, bias_ref, *, base, shift, scale):
    qb = pl.program_id(1)
    n_heads = q_ref.shape[1] // 128
    per_part = base // BK
    q_first = base + qb * BQ
    m_ref[...] = jnp.full(m_ref.shape, NEG, jnp.float32)
    l_ref[...] = jnp.zeros(l_ref.shape, jnp.float32)
    acc_ref[...] = jnp.zeros(acc_ref.shape, jnp.float32)

    def process(kb, masked):
        k_first = kb * BK
        part = kb // per_part
        stored = part * per_part + lax.rem(kb - part * per_part + shift // BK, per_part)
        k_rows = pl.ds(pl.multiple_of(stored * BK, BK), BK)
        k_blk = k_ref[k_rows, :]
        v_blk = v_ref[k_rows, :]
        if masked:
            k_idx = k_first + lax.broadcasted_iota(jnp.int32, (BQ, BK), 1)
            q_idx = q_first + lax.broadcasted_iota(jnp.int32, (BQ, BK), 0)
            ok = (k_idx >= lo_ref[...]) & (k_idx <= q_idx)
            bias_ref[...] = jnp.where(ok, 0.0, NEG)

        def score(n):
            return lax.dot_general(q_ref[:, n * 128:(n + 1) * 128], k_blk, (((1,), (1,)), ((), ())), preferred_element_type=jnp.float32)

        s_next = score(0)
        for n in range(n_heads):
            s = s_next
            if n + 1 < n_heads:
                s_next = score(n + 1)
            if masked:
                s = s + bias_ref[...]
            m_old = m_ref[n]
            m_new = jnp.maximum(m_old, jnp.max(s, axis=1, keepdims=True))
            alpha = jnp.exp2((m_old - m_new) * scale)
            p = jnp.exp2((s - jnp.concatenate([m_new] * (BK // 128), axis=1)) * scale)
            p_sum = p[:, :128]
            for c in range(128, BK, 128):
                p_sum = p_sum + p[:, c:c + 128]
            l_ref[n] = l_ref[n] * alpha + p_sum
            m_ref[n] = m_new
            pv = jnp.dot(p.astype(jnp.bfloat16), v_blk, preferred_element_type=jnp.float32)
            acc_ref[n] = acc_ref[n] * alpha + pv

    first = lomin_ref[qb] // BK
    last = (q_first + BQ - 1) // BK
    full_from = lomax_ref[qb]

    def step(kb, carry):
        inside = (kb * BK >= full_from) & ((kb + 1) * BK - 1 <= q_first)

        @pl.when(inside)
        def _():
            process(kb, False)

        @pl.when(jnp.logical_not(inside))
        def _():
            process(kb, True)

        return carry

    lax.fori_loop(first, last + 1, step, 0)
    for n in range(n_heads):
        o_ref[:, n * 128:(n + 1) * 128] = (acc_ref[n] / jnp.sum(l_ref[n], axis=1, keepdims=True)).astype(jnp.bfloat16)


def flash(q, kv, lo, shift):
    n_rows, width = q.shape
    n_kv = kv.shape[1] // 256
    group = width // n_kv
    n_q = n_rows // BQ
    blocks = lo.reshape(n_q, BQ)
    n_h = group // 128

    def q_at(h, i, *_):
        return lax.rem(i + shift // BQ, n_q), h

    return pl.pallas_call(
        functools.partial(flash_kernel, base=n_rows, shift=shift, scale=(128 ** -0.5) * LOG2E),
        grid_spec=pltpu.PrefetchScalarGridSpec(
            num_scalar_prefetch=2,
            grid=(n_kv, n_q),
            in_specs=[
                pl.BlockSpec((BQ, 1), lambda h, i, *_: (i, 0)),
                pl.BlockSpec((BQ, group), q_at),
                pl.BlockSpec((2 * n_rows, 128), lambda h, i, *_: (0, h)),
                pl.BlockSpec((2 * n_rows, 128), lambda h, i, *_: (0, n_kv + h)),
            ],
            out_specs=pl.BlockSpec((BQ, group), q_at),
            scratch_shapes=[
                pltpu.VMEM((n_h, BQ, 128), jnp.float32),
                pltpu.VMEM((n_h, BQ, 128), jnp.float32),
                pltpu.VMEM((n_h, BQ, 128), jnp.float32),
                pltpu.VMEM((BQ, BK), jnp.float32),
            ],
        ),
        out_shape=jax.ShapeDtypeStruct((n_rows, width), jnp.bfloat16),
        compiler_params=pltpu.CompilerParams(dimension_semantics=("arbitrary", "arbitrary")),
        cost_estimate=pl.CostEstimate(flops=80_000_000_000, bytes_accessed=40_000_000, transcendentals=80_000_000),
        name="flash",
    )(jnp.min(blocks, axis=1), jnp.max(blocks, axis=1), lo[:, None], q, kv, kv)


def ring_perm(n_dev, shift):
    order = ring_order(n_dev)
    return [(order[r], order[(r + shift) % n_dev]) for r in range(n_dev)]


def ring_order(n_dev):
    return [0, 1, 2, 3, 6, 7, 4, 5]


def ring_plan(send_len_all, n_cap):
    n_dev = send_len_all.shape[0]
    totals = jnp.sum(send_len_all, axis=1)
    totals = jnp.stack([totals[d] for d in ring_order(n_dev)])
    ends = jnp.cumsum(totals)
    excess = ends - totals - n_cap * jnp.arange(n_dev, dtype=jnp.int32)
    centre = (jnp.max(excess) + jnp.min(excess)) // 2
    return totals, ends - totals, centre - excess


def balanced_path(plan, hidden, g_attn, w_q, w_k, w_v, w_o, g_mlp, w_gate, w_up, w_down):
    ext_idx, back_k, pos, n_left, n_right, bucket = plan
    n_tok, model_dim = hidden.shape
    n_cap = pos.shape[0]
    n_dev = 8
    head = HEAD_ROWS
    up, down = ring_perm(n_dev, 1), ring_perm(n_dev, -1)
    slot = jnp.arange(n_cap, dtype=jnp.int32)[:, None]
    levels = LEVELS

    def grab(idx):
        return hidden.at[idx].get(mode='promise_in_bounds')

    def exchange(cap):
        def run():
            sent = grab(jnp.concatenate([ext_idx[n_cap - cap:n_cap], ext_idx[2 * n_cap:2 * n_cap + cap]]))
            right = lax.ppermute(sent[:cap], 'sp', down)
            left = lax.ppermute(sent[cap:], 'sp', up)
            own = grab(ext_idx[n_cap:2 * n_cap])
            pad = jnp.zeros((n_cap - cap, model_dim), hidden.dtype)
            left = jnp.concatenate([left, pad], axis=0)
            right = jnp.concatenate([pad, right], axis=0)

            def pick(a, b):
                return jnp.where(slot[a:b] < n_left, left[a:b], jnp.where(slot[a:b] >= n_cap - n_right, right[a:b], own[a:b]))

            return jnp.concatenate([pick(n_cap - head, n_cap), pick(0, n_cap - head)], axis=0)
        return run

    rows = row_major(lax.switch(bucket, [exchange(cap) for cap in levels]))
    normed = row_major(rms_norm(rows, g_attn))
    tables = lax.optimization_barrier(rope_tables(jnp.roll(pos, head), w_q.shape[2]))
    n_kv, head_dim = w_k.shape[1:]
    w_kv = jnp.concatenate([w_k.reshape(model_dim, -1), w_v.reshape(model_dim, -1)], axis=1)
    kv_proj = row_major(jnp.dot(normed, w_kv, preferred_element_type=jnp.float32))
    kv_width = n_kv * head_dim

    def turn(proj):
        return rope(proj.reshape(n_cap, -1, head_dim), tables).astype(jnp.bfloat16).reshape(n_cap, -1)

    kv = row_major(jnp.concatenate([turn(kv_proj[:, :kv_width]), kv_proj[:, kv_width:].astype(jnp.bfloat16)], axis=1))
    kv_prev = lax.ppermute(kv, 'sp', up)
    q_proj = row_major(jnp.dot(normed, w_q.reshape(model_dim, -1), preferred_element_type=jnp.float32))
    q_rot = row_major(turn(q_proj))
    kv = jnp.concatenate([kv_prev, kv], axis=0)
    heads = flash(q_rot, kv, n_cap + slot[:, 0] - pos, head)
    resid_mid = row_major(attn_residual(rows, heads, w_o))
    ends = row_major(mlp_residual(resid_mid[:2 * head], g_mlp, w_gate, w_up, w_down))
    from_next = lax.ppermute(ends[head:], 'sp', down)
    from_prev = lax.ppermute(ends[:head], 'sp', up)
    resid_tail = lax.optimization_barrier((resid_mid[2 * head:], ends[:8]))[0]
    middle = row_major(mlp_residual(resid_tail, g_mlp, w_gate, w_up, w_down))

    def give_back(cap):
        extra = max(cap - head, 0)

        def run():
            parts = [ends, middle, from_next, from_prev]
            stored = lax.rem(back_k + head, n_cap)
            place = jnp.where((back_k >= 0) & (back_k < n_cap), stored, 0)
            place = jnp.where((back_k >= n_cap) & (back_k < n_cap + head), back_k, place)
            place = jnp.where((back_k < 0) & (back_k >= -head), n_cap + 2 * head + back_k, place)
            size = n_cap + 2 * head
            if extra:
                over = max(cap + head - n_cap, 0)
                n_mid = extra - over
                parts.append(lax.ppermute(jnp.concatenate([middle[:n_mid], ends[:over]], axis=0), 'sp', down))
                parts.append(lax.ppermute(jnp.concatenate([ends[2 * head - over:], middle[middle.shape[0] - n_mid:]], axis=0), 'sp', up))
                place = jnp.where((back_k >= n_cap + head) & (back_k < n_cap + cap), size + back_k - n_cap - head, place)
                place = jnp.where((back_k < -head) & (back_k >= -cap), size + 2 * extra + head + back_k, place)
                size += 2 * extra
            parts.append(jnp.zeros((16, model_dim), hidden.dtype))
            place = jnp.where((back_k < -cap) | (back_k >= n_cap + cap), size, place)
            return jnp.concatenate(parts, axis=0).at[place].get(mode='promise_in_bounds')
        return run

    return lax.switch(bucket, [give_back(cap) for cap in levels])


def solution(mesh):
    row_spec = P(('dp', 'sp'), None)
    vec_spec = P(('dp', 'sp'))
    rep_spec = P()

    def per_device(hidden, tok_perm, send_off, send_len, recv_off, recv_len, recv_doc, recv_pos, *params):
        n_tok = hidden.shape[0]
        n_cap = recv_doc.shape[0]
        n_dev = send_off.shape[0]
        at_start = jnp.arange(n_cap, dtype=jnp.int32)[None, :] == recv_off[:, None]
        start_pos = jnp.sum(jnp.where(at_start, recv_pos[None, :], 0), axis=1)
        broken = jnp.sum(jnp.where(recv_len > 0, start_pos, 0))
        mine = jnp.concatenate([recv_pos, send_len, recv_off, jnp.full((112,), broken, jnp.int32)])
        every = lax.all_gather(mine, 'sp', axis=0)
        pos_all = every[:, :n_cap]
        send_all = every[:, n_cap:n_cap + n_dev]
        roff_all = every[:, n_cap + n_dev:n_cap + 2 * n_dev]
        totals, starts, offs = ring_plan(send_all, n_cap)
        prev_totals = jnp.concatenate([totals[-1:], totals[:-1]])
        fits = jnp.all((offs >= -prev_totals) & (offs <= totals) & (jnp.abs(offs) <= n_cap))
        whole = jnp.sum(jnp.abs(every[:, n_cap + 2 * n_dev])) == 0
        use_ring = fits & whole

        me = lax.axis_index('sp').astype(jnp.int32)
        ring_at = jnp.where(me < 4, me, me ^ 2)
        after = lax.rem(ring_at + 1, n_dev)
        off = jnp.clip(offs[ring_at], -n_cap, n_cap)
        off_next = jnp.clip(offs[after], -n_cap, n_cap)
        total = totals[ring_at]
        ext_idx = lax.dynamic_slice(jnp.pad(tok_perm, (2 * n_cap, 2 * n_cap)), (n_cap + off,), (3 * n_cap,))
        n_left = jnp.maximum(-off, 0)
        n_right = jnp.maximum(off_next, 0)
        order = jnp.argsort(tok_perm)
        back_k = jnp.where(order < total, order - off, 4 * n_cap).astype(jnp.int32)
        reach = jnp.max(jnp.abs(offs))
        bucket = sum((reach > level).astype(jnp.int32) for level in LEVELS[:-1])

        order_of = ring_order(n_dev)
        runs = jnp.stack([send_all[d] for d in order_of])
        run_slot = jnp.stack([roff_all[:, d] for d in order_of])
        run_rel = starts[:, None] + jnp.cumsum(runs, axis=1) - runs - starts[ring_at] - off
        half = n_dev * n_cap // 2
        run_rel = jnp.where(run_rel >= half, run_rel - 2 * half, jnp.where(run_rel < -half, run_rel + 2 * half, run_rel))
        in_run = jnp.arange(n_cap, dtype=jnp.int32)[:, None] - run_rel.reshape(1, -1)
        run_base = (jnp.arange(n_dev, dtype=jnp.int32)[None, :] * every.shape[1] + run_slot).reshape(1, -1)
        from_at = jnp.sum(jnp.where((in_run >= 0) & (in_run < runs.reshape(1, -1)), run_base + in_run, 0), axis=1)
        pos = every.reshape(-1).at[from_at].get(mode='promise_in_bounds')

        plan = (ext_idx, back_k, pos, n_left, n_right, bucket)

        def ring(_):
            return balanced_path(plan, hidden, *params)

        def general(_):
            return general_path(hidden, tok_perm, send_off, send_len, recv_off, recv_len, recv_doc, recv_pos, *params)

        return lax.cond(use_ring, ring, general, 0)

    return jax.shard_map(per_device, mesh=mesh, in_specs=(row_spec,) + (vec_spec,) * 7 + (rep_spec,) * 9, out_specs=row_spec, check_vma=False)
```

time: 4600 us -> 1300 us (0.28)
  waiting for transfers between devices: 2130 us -> 82.2 us
  local copies, waits for them, and re-layouts: 994 us -> 253 us
  matrix products: 1220 us -> 586 us
  Pallas kernels: 0 us -> 209 us
  other arithmetic: 212 us -> 121 us
    all_to_all x2 -> x0, waiting for transfers between devices: 2130 us -> none  [the longest x1 1070 us: per_device(): lax.all_to_all(back_buf, 'sp', 0, 0, tiled=True)]
    gather x7 -> x6, local copies, waits for them, and re-layouts: 894 us -> 157 us  [the longest x2 78.2 us: grab(): return hidden.at[idx].get(mode='promise_in_bounds')]
    sub x24 -> x0, matrix products: 359 us -> none  [one_block(): jax.nn.softmax(jnp.where(allowed, scores, -1e+30), axis=-1)]
    dot_general x29 -> x9, matrix products: 815 us -> 586 us  [the longest x2 185 us: mlp_residual(): up_proj = jnp.dot(normed_mlp, w_up, preferred_element_type=jnp.float32)]
    pallas_call x0 -> x1, Pallas kernels: none -> 209 us  [flash(): pl.pallas_call(functools.partial(flash_kernel, base=n_rows, shift=shift,...]
    select_n x8 -> x6, other arithmetic: 153 us -> 13.9 us  [the longest x2 12 us: pick(): jnp.where(slot[a:b] < n_left, left[a:b], jnp.where(slot[a:b] >= n_cap - n...]
    ppermute x0 -> x7, waiting for transfers between devices: none -> 82.2 us  [the longest x1 56.2 us: run(): right = lax.ppermute(sent[:cap], 'sp', down)]
    cond x0 -> x63, local copies, waits for them, and re-layouts: none -> 62.5 us
  transfers between devices with their start and end apart: 2 -> 7, of which waited for: 2 -> 2; matrix products, arithmetic and copies ran while one was open for 1% -> 18% of each run, Pallas kernels for 0% -> 0%
where the time goes in v1:
time: 1300 us
  matrix products  586 us (45%)
  local copies, waits for them, and re-layouts  253 us (19%)
  Pallas kernels  209 us (16%)
  other arithmetic  121 us (9%)
  waiting for transfers between devices  82.2 us (6%)
  loops' own time  27.4 us (2%)
    pallas_call x1, Pallas kernels, flash(): pl.pallas_call(functools.partial(flash_kernel, base=n_rows, shift=shift,...  209 us
    dot_general x2, matrix products, mlp_residual(): up_proj = jnp.dot(normed_mlp, w_up, preferred_element_type=jnp.float32)  185 us
    dot_general x2, matrix products, mlp_residual(): jnp.dot(hidden_act, w_down, preferred_element_type=jnp.float32)  166 us
    dot_general x2, matrix products, mlp_residual(): gate_proj = jnp.dot(normed_mlp, w_gate, preferred_element_type=jnp.float32)  159 us
    gather x2, local copies, waits for them, and re-layouts, grab(): return hidden.at[idx].get(mode='promise_in_bounds')  78.2 us
    cond x63, local copies, waits for them, and re-layouts  62.5 us
    gather x1, local copies, waits for them, and re-layouts, run(): jnp.concatenate(parts, axis=0).at[place].get(mode='promise_in_bounds')  59.5 us
    ppermute x1, waiting for transfers between devices, run(): right = lax.ppermute(sent[:cap], 'sp', down)  56.2 us
  transfers between devices with their start and end apart: 7, of which 2 were waited for; matrix products, arithmetic and copies ran while one was open for 18% of the time, Pallas kernels for 0%

profile of v1, /device:TPU:3, one launch (start us, length us, event | category | flops | bytes accessed | tf_op | source)
XLA Modules:
  0.0 1299.7 jit_solution(11815642338425000769)
XLA Ops:
  0.0 0.9 select_reduce_fusion.3
  0.9 1.3 fusion.127
  2.9 0.8 concatenate.194
  3.7 10.2 all-gather.1
  14.5 0.8 slice_reduce_fusion.8
  20.3 1.9 slice_reduce_fusion
  24.4 7.4 sort.31
  32.5 1.4 and_reduce_fusion
  35.1 1263.5 %conditional.3 = (bf16[6144,2048]{1,0:T(8,128)(2,1)}) conditional(s32[]{:T(128)} %convert_element_type.150, (s32[6144]{0:T(1024)}, s32[8]{0:T(128)}, s32[8]{0:T(128)}, s32[8]{0:T(128)}, s32[8]{0:T(128)}, /*index=5*/bf16[6144,2048]{1,0:T(8,128)(2,1)}, bf16[2048]{0:T(1024)(128)(2,1)}, bf16[2048,16,128]{2,1,0:T(8,128)(2,1)}, s32[3072]{0:T(1024)}, ...), branch_computations={%region_11.22_spmd, %region_22.37_spmd} | conditional | flops 554083483648 | bytes 2587438592 | solution.py:372
  40.6 1.2 dynamic_slice.27
  44.6 0.9 reshape.766
  45.5 17.4 %gather_fusion.12 = s32[3072]{0:T(1024)S(1)} fusion(s32[25600]{0:T(1024)S(1)} %reshape.766, s32[3072]{0:T(1024)S(1)} %broadcast_clamp_fusion.9), kind=kCustom, calls=%fused_computation.17 | custom fusion | bytes 36864 | tf_op jit(solution)/shard_map/gather | solution.py:362
  64.9 189.3 %conditional = (bf16[3072,2048]{1,0:T(8,128)(2,1)}) conditional(s32[]{:T(128)} %clamp.0, (s32[3072,1]{0,1:T(1,128)S(1)}, s32[3072,1]{0,1:T(1,128)S(1)}, s32[]{:T(128)}, s32[]{:T(128)}, s32[9216]{0:T(1024)S(1)}, /*index=5*/bf16[6144,2048]{1,0:T(8,128)(2,1)}, s32[3072,1]{0,1:T(1,128)S(1)}, ...), branch_computations={%region_23.23_spmd, %region_24.24_spmd, %region_25.25_spmd, %regio... | conditional | flops 37797888 | bytes 352567392 | solution.py:266
  68.2 43.0 %gather_fusion.8 = bf16[4096,2048]{1,0:T(8,128)(2,1)} fusion(bf16[6144,2048]{1,0:T(8,128)(2,1)} %get-tuple-element.409, s32[4096]{0:T(1024)S(1)} %broadcast_clamp_fusion.7), kind=kCustom, calls=%fused_computation.9 | custom fusion | bytes 33570816 | tf_op jit(solution)/shard_map/cond/branch_1_fun/cond/branch_2_fun/gather | solution.py:248
  111.2 11.9 fusion.145
  123.1 1.5 collective-permute-start.10
  124.6 1.1 collective-permute-start.11
  125.7 35.2 %gather_fusion.9 = bf16[3072,2048]{1,0:T(8,128)(2,1)} fusion(bf16[6144,2048]{1,0:T(8,128)(2,1)} %get-tuple-element.409, s32[3072]{0:T(1024)S(1)} %fusion.87), kind=kCustom, calls=%fused_computation.10 | custom fusion | bytes 25178112 | tf_op jit(solution)/shard_map/cond/branch_1_fun/cond/branch_2_fun/gather | solution.py:248
  161.0 56.2 %collective-permute-done.10 = bf16[2048,2048]{1,0:T(8,128)(2,1)} collective-permute-done((bf16[2048,2048]{1,0:T(8,128)(2,1)}, bf16[2048,2048]{1,0:T(8,128)(2,1)}, u32[]{:S(2)}, u32[]{:S(2)}) %collective-permute-start.10) | collective-permute-done | bytes 8388640 | tf_op jit(solution)/shard_map/cond/branch_1_fun/cond/branch_2_fun/ppermute | solution.py:253
  217.2 4.0 fusion.86
  221.2 8.0 fusion.85
  229.2 14.9 %pad_maximum_fusion.6 = bf16[3072,2048]{1,0:T(8,128)(2,1)} fusion(bf16[2048,2048]{1,0:T(8,128)(2,1)S(1)} %fusion.85, bf16[1024,2048]{1,0:T(8,128)(2,1)S(1)} %fusion.86), kind=kLoop, calls=%fused_computation.191 | loop fusion | flops 25165824 | bytes 25165824 | tf_op jit(solution)/shard_map/cond/branch_1_fun/cond/branch_2_fun/concatenate | solution.py:263
  254.2 7.2 fusion.91
  261.9 9.6 fusion.108
  271.5 2.0 slice.396
  273.6 1.4 slice.514
  274.9 3.5 reshape.771
  278.5 5.5 multiply_sine_fusion.1
  284.0 8.5 subtract_convert_fusion.3
  292.5 4.8 pad_maximum_fusion.10
  297.5 1.9 pad_maximum_fusion.9
  299.4 34.3 %convolution_bitcast_fusion = f32[384,8,16,128]{3,1,2,0:T(8,128)} fusion(bf16[256,8,16,128]{3,2,1,0:T(8,128)(2,1)} %bitcast.210, bf16[3072,2048]{1,0:T(8,128)(2,1)} %get-tuple-element.846, f32[2048]{0:T(1024)S(1)} %convert_element_type.125, f32[3072]{0:T(1024)S(1)} %add_rsqrt_fusion.2), kind=kOutput, calls=%fused_computation.243 | convolution fusion | flops 25794969600 | bytes 46157824 | tf_op jit(solution)/shard_map/cond/branch_1_fun/dot_general | solution.py:279
  333.7 21.1 %copy.121 = f32[384,8,16,128]{3,2,1,0:T(8,128)} copy(f32[384,8,16,128]{3,1,2,0:T(8,128)} %convolution_bitcast_fusion) | data formatting | bytes 50331648 | tf_op jit(solution)/shard_map/cond
  354.8 25.2 %subtract_convert_fusion.2 = (bf16[3072,16,64]{2,1,0:T(8,128)(2,1)S(1)}, bf16[3072,16,64]{2,1,0:T(8,128)(2,1)}) fusion(f32[3072,16,128]{2,1,0:T(8,128)} %bitcast.200, f32[3072,64]{1,0:T(8,128)S(1)} %copy-done.16, f32[3072,64]{1,0:T(8,128)S(1)} %copy-done.18), kind=kLoop, calls=%fused_computation.231 | loop fusion | flops 25165824 | bytes 39321600 | tf_op jit(solution)/shard_map/convert.3
  380.1 9.6 pad_maximum_fusion.8
  389.7 7.1 copy.138
  396.8 1.7 copy.101
  400.5 1.2 subtract_select_fusion
  401.7 2.8 add_subtract_fusion.lo_ref
  404.5 4.9 maximum_maximum_fusion.k_ref.v_ref
  409.4 208.9 %flash.1 = bf16[3072,2048]{1,0:T(8,128)(2,1)} custom-call(s32[6]{0:T(128)} %get-tuple-element.651.lomin_ref, s32[6]{0:T(128)} %get-tuple-element.650.lomax_ref, s32[3072,1]{1,0:T(8,128)} %add_subtract_fusion.lo_ref, bf16[3072,2048]{1,0:T(8,128)(2,1)} %bitcast.209, bf16[6144,512]{1,0:T(8,128)(2,1)} %maximum_maximum_fusion.k_ref.v_ref, ...), custom_call_target="tpu_custom_call" | custom-call | flops 80000000000 | bytes 40000000 | tf_op jit(solution)/shard_map/cond/branch_1_fun/flash/pallas_call | solution.py:192
  618.3 32.1 %fusion.94 = bf16[3072,2048]{1,0:T(8,128)(2,1)S(1)} fusion(bf16[3072,2048]{1,0:T(8,128)(2,1)} %get-tuple-element.846, bf16[3072,2048]{1,0:T(8,128)(2,1)} %flash.1, bf16[2048,2048]{1,0:T(8,128)(2,1)} %bitcast.259), kind=kOutput, calls=%fused_computation.226 | convolution fusion | flops 25801261056 | bytes 46137344 | tf_op jit(solution)/shard_map/cond/branch_1_fun/dot_general | solution.py:74
  650.7 1.8 fusion.96
  652.5 0.9 fusion.101
  653.8 0.8 copy-done.50
  654.6 55.7 %fusion.119 = f32[1024,11008]{1,0:T(8,128)} fusion(bf16[2048,11008]{1,0:T(8,128)(2,1)} %get-tuple-element.465, bf16[1024,2048]{1,0:T(8,128)(2,1)S(1)} %slice.401, f32[2048]{0:T(1024)S(1)} %copy-done.48, f32[1024]{0:T(1024)S(1)} %add_rsqrt_fusion.4), kind=kOutput, calls=%fused_computation.266 | convolution fusion | flops 46179287040 | bytes 94384128 | tf_op jit(solution)/shard_map/cond/branch_1_fun/dot_general | solution.py:80
  710.4 103.7 %fusion.115 = f32[2048,11008]{1,0:T(8,128)} fusion(bf16[2048,11008]{1,0:T(8,128)(2,1)} %get-tuple-element.465, f32[2048]{0:T(1024)S(1)} %copy-done.48, f32[2048]{0:T(1024)S(1)} %add_rsqrt_fusion.3, bf16[3072,2048]{1,0:T(8,128)(2,1)S(1)} %fusion.94), kind=kOutput, calls=%fused_computation.265 | convolution fusion | flops 92358574080 | bytes 143671296 | tf_op jit(solution)/shard_map/cond/branch_1_fun/dot_general | solution.py:80
  814.1 63.8 %multiply_convert_fusion.2.clone.6 = bf16[1024,11008]{1,0:T(8,128)(2,1)} fusion(f32[1024,11008]{1,0:T(8,128)} %fusion.119, bf16[2048,11008]{1,0:T(8,128)(2,1)} %get-tuple-element.466, bf16[1024,2048]{1,0:T(8,128)(2,1)} %copy-done.12, f32[2048]{0:T(1024)S(1)} %copy-done.48, f32[1024]{0:T(1024)S(1)} %copy-done.51), kind=kOutput, calls=%fused_computation.219.clone.clone.clone.clone.clone.1 | convolution fusion | flops 46246920192 | bytes 116928512 | tf_op jit(solution)/shard_map/cond/branch_1_fun/dot_general | solution.py:81
  877.9 121.0 %multiply_convert_fusion.1.clone.6 = bf16[2048,11008]{1,0:T(8,128)(2,1)} fusion(f32[2048,11008]{1,0:T(8,128)} %fusion.115, bf16[2048,11008]{1,0:T(8,128)(2,1)} %get-tuple-element.466, f32[2048]{0:T(1024)S(1)} %copy-done.48, f32[2048]{0:T(1024)S(1)} %add_rsqrt_fusion.3, bf16[3072,2048]{1,0:T(8,128)(2,1)} %copy-done.19), kind=kOutput, calls=%fused_computation.218.clone.clone.clone.clone.clone.1 | convolution fusion | flops 92493840384 | bytes 188760064 | tf_op jit(solution)/shard_map/cond/branch_1_fun/dot_general | solution.py:81
  998.9 106.5 %fusion.99 = bf16[2048,2048]{1,0:T(8,128)(2,1)S(1)} fusion(bf16[11008,2048]{1,0:T(8,128)(2,1)} %get-tuple-element.467, bf16[3072,2048]{1,0:T(8,128)(2,1)} %copy-done.19, bf16[2048,11008]{1,0:T(8,128)(2,1)} %multiply_convert_fusion.1.clone.6), kind=kOutput, calls=%fused_computation.236 | convolution fusion | flops 92362768384 | bytes 106954752 | tf_op jit(solution)/shard_map/cond/branch_1_fun/dot_general | solution.py:83
  1105.4 3.2 copy-done.3
  1108.6 3.8 fusion.149
  1112.4 1.7 collective-permute-start.16
  1114.1 59.1 %fusion.104 = bf16[1024,2048]{1,0:T(8,128)(2,1)} fusion(bf16[1024,2048]{1,0:T(8,128)(2,1)} %copy-done.12, bf16[11008,2048]{1,0:T(8,128)(2,1)} %get-tuple-element.467, bf16[1024,11008]{1,0:T(8,128)(2,1)} %multiply_convert_fusion.2.clone.6), kind=kOutput, calls=%fused_computation.247 | convolution fusion | flops 46181384192 | bytes 76021760 | tf_op jit(solution)/shard_map/cond/branch_1_fun/dot_general | solution.py:83
  1173.2 124.6 %conditional.1 = (bf16[6144,2048]{1,0:T(8,128)(2,1)}) conditional(s32[]{:T(128)} %clamp.0, (bf16[2048,2048]{1,0:T(8,128)(2,1)}, bf16[1024,2048]{1,0:T(8,128)(2,1)}, bf16[1024,2048]{1,0:T(8,128)(2,1)}, bf16[1024,2048]{1,0:T(8,128)(2,1)}, s32[6144]{0:T(1024)S(1)}) %tuple.216, (bf16[1024,2048]{1,0:T(8,128)(2,1)}, ...), branch_computations={%region_33.33_spmd, %region_34.34_spmd, %region_35.35_spmd, %regio... | conditional | flops 33751040 | bytes 255991904 | solution.py:313
  1179.5 1.7 collective-permute-start.1
  1181.2 8.3 constant_dynamic-update-slice_fusion.15
  1189.6 2.2 constant_dynamic-update-slice_fusion.14
  1191.8 4.8 constant_dynamic-update-slice_fusion.13
  1196.6 4.7 constant_dynamic-update-slice_fusion.12
  1201.4 26.0 %collective-permute-done = bf16[1024,2048]{1,0:T(8,128)(2,1)} collective-permute-done((bf16[1024,2048]{1,0:T(8,128)(2,1)}, bf16[1024,2048]{1,0:T(8,128)(2,1)}, u32[]{:S(2)}, u32[]{:S(2)}) %collective-permute-start) | collective-permute-done | bytes 4194336 | tf_op jit(solution)/shard_map/cond/branch_1_fun/cond/branch_2_fun/ppermute | solution.py:303
  1227.4 4.7 constant_dynamic-update-slice_fusion.11
  1232.1 4.7 constant_dynamic-update-slice_fusion.10
  1237.4 59.5 %gather_fusion.1 = bf16[6144,2048]{1,0:T(8,128)(2,1)} fusion(bf16[7184,2048]{1,0:T(8,128)(2,1)} %broadcast_dynamic-update-slice_fusion.2, s32[6144]{0:T(1024)S(1)} %fusion.75), kind=kCustom, calls=%fused_computation.15 | custom fusion | bytes 50356224 | tf_op jit(solution)/shard_map/cond/branch_1_fun/cond/branch_2_fun/gather | solution.py:310
  (122 shorter events, 14.6 us)
Async XLA Ops:
  15.5 19.6 %copy-start.45 = (s32[8]{0:T(128)}, s32[8]{0:T(128)S(1)}, u32[]{:S(2)}) copy-start(s32[8]{0:T(128)S(1)} %pad_add_fusion.1) | copy-start | bytes 100
  16.4 6.7 copy-start.49
  23.7 0.6 copy-start.34
  39.3 3.1 copy-start.54
  39.3 25.4 %copy-start.2 = (s32[6144]{0:T(1024)S(1)}, s32[6144]{0:T(1024)}, u32[]{:S(2)}) copy-start(s32[6144]{0:T(1024)} %get-tuple-element.447) | copy-start | bytes 73732 | tf_op jit(solution)/shard_map/cond
  42.5 21.0 %copy-start.55 = (s32[8]{0:T(128)S(1)}, s32[8]{0:T(128)}, u32[]{:S(2)}) copy-start(s32[8]{0:T(128)} %copy-done.54) | copy-start | bytes 100 | tf_op jit(solution)/shard_map/cond
  62.9 2.0 copy-start.30
  123.1 94.1 %collective-permute-start.10 = (bf16[2048,2048]{1,0:T(8,128)(2,1)}, bf16[2048,2048]{1,0:T(8,128)(2,1)}, u32[]{:S(2)}, u32[]{:S(2)}) collective-permute-start(bf16[2048,2048]{1,0:T(8,128)(2,1)} %get-tuple-element.718), channel_id=1, source_target_pairs={{0,5},{1,0},{2,1},{3,2},{6,3},{7,6},{4,7},{5,4}} | collective-permute-start | bytes 25165832 | tf_op jit(solution)/shard_map/cond/branch_1_fun/cond/branch_2_fun/ppermute | solution.py:253
  124.6 96.6 %collective-permute-start.11 = (bf16[2048,2048]{1,0:T(8,128)(2,1)}, bf16[2048,2048]{1,0:T(8,128)(2,1)}, u32[]{:S(2)}, u32[]{:S(2)}) collective-permute-start(bf16[2048,2048]{1,0:T(8,128)(2,1)} %get-tuple-element.719), channel_id=1, source_target_pairs={{0,1},{1,2},{2,3},{3,6},{6,7},{7,4},{4,5},{5,0}} | collective-permute-start | bytes 25165832 | tf_op jit(solution)/shard_map/cond/branch_1_fun/cond/branch_2_fun/ppermute | solution.py:254
  160.9 60.3 %copy-start.9 = (bf16[3072,2048]{1,0:T(8,128)(2,1)S(1)}, bf16[3072,2048]{1,0:T(8,128)(2,1)}, u32[]{:S(2)}) copy-start(bf16[3072,2048]{1,0:T(8,128)(2,1)} %gather_fusion.9) | copy-start | bytes 37748740 | tf_op jit(solution)/shard_map/cond/branch_1_fun/cond
  254.2 7.3 copy-start.37
  254.2 7.3 copy-start.21
  254.2 7.3 copy-start.24
  271.5 7.0 slice-start
  271.5 7.0 slice-start.1
  271.5 7.0 copy-start.57
  278.5 19.0 %copy-start.13 = (bf16[3072,256]{1,0:T(8,128)(2,1)S(1)}, bf16[3072,256]{1,0:T(8,128)(2,1)}, u32[]{:S(2)}) copy-start(bf16[3072,256]{1,0:T(8,128)(2,1)} %slice.514) | copy-start | bytes 4718596 | tf_op jit(solution)/shard_map/cond
  284.0 15.4 %copy-start.15 = (f32[3072,64]{1,0:T(8,128)}, f32[3072,64]{1,0:T(8,128)S(1)}, u32[]{:S(2)}) copy-start(f32[3072,64]{1,0:T(8,128)S(1)} %get-tuple-element.460) | copy-start | bytes 2359300 | tf_op jit(solution)/shard_map/cond
  284.0 15.4 %copy-start.17 = (f32[3072,64]{1,0:T(8,128)}, f32[3072,64]{1,0:T(8,128)S(1)}, u32[]{:S(2)}) copy-start(f32[3072,64]{1,0:T(8,128)S(1)} %get-tuple-element.459) | copy-start | bytes 2359300 | tf_op jit(solution)/shard_map/cond
  284.0 15.4 %copy-start.31 = (s32[3072]{0:T(1024)S(1)}, s32[3072]{0:T(1024)}, u32[]{:S(2)}) copy-start(s32[3072]{0:T(1024)} %copy-done.30) | copy-start | bytes 36868 | tf_op jit(solution)/shard_map/cond
  299.4 105.1 %collective-permute-start.14 = (bf16[3072,512]{1,0:T(8,128)(2,1)}, bf16[3072,512]{1,0:T(8,128)(2,1)}, u32[]{:S(2)}, u32[]{:S(2)}) collective-permute-start(bf16[3072,512]{1,0:T(8,128)(2,1)} %pad_maximum_fusion.9), channel_id=1, source_target_pairs={{0,1},{1,2},{2,3},{3,6},{6,7},{7,4},{4,5},{5,0}} | collective-permute-start | bytes 9437192 | tf_op jit(solution)/shard_map/cond/branch_1_fun/ppermute | solution.py:278
  333.7 21.1 %copy-start.16 = (f32[3072,64]{1,0:T(8,128)S(1)}, f32[3072,64]{1,0:T(8,128)}, u32[]{:S(2)}) copy-start(f32[3072,64]{1,0:T(8,128)} %copy-done.15) | copy-start | bytes 2359300 | tf_op jit(solution)/shard_map/cond
  333.7 21.1 %copy-start.18 = (f32[3072,64]{1,0:T(8,128)S(1)}, f32[3072,64]{1,0:T(8,128)}, u32[]{:S(2)}) copy-start(f32[3072,64]{1,0:T(8,128)} %copy-done.17) | copy-start | bytes 2359300 | tf_op jit(solution)/shard_map/cond
  389.7 8.8 copy-start.39
  389.7 9.4 copy-start.46
  389.7 10.8 copy-start.35
  389.7 14.8 %copy-start.14 = (bf16[3072,256]{1,0:T(8,128)(2,1)S(1)}, bf16[3072,256]{1,0:T(8,128)(2,1)}, u32[]{:S(2)}) copy-start(bf16[3072,256]{1,0:T(8,128)(2,1)} %slice.514) | copy-start | bytes 4718596 | tf_op jit(solution)/shard_map/cond
  650.4 60.0 %copy-start.19 = (bf16[3072,2048]{1,0:T(8,128)(2,1)}, bf16[3072,2048]{1,0:T(8,128)(2,1)S(1)}, u32[]{:S(2)}) copy-start(bf16[3072,2048]{1,0:T(8,128)(2,1)S(1)} %fusion.94) | copy-start | bytes 37748740 | tf_op jit(solution)/shard_map/cond
  650.4 4.2 copy-start.48
  650.7 3.1 copy-start.12
  653.4 1.2 copy-start.50
  710.4 103.7 %copy-start.51 = (f32[1024]{0:T(1024)S(1)}, f32[1024]{0:T(1024)}, u32[]{:S(2)}) copy-start(f32[1024]{0:T(1024)} %copy-done.50) | copy-start | bytes 12292 | tf_op jit(solution)/shard_map/cond
  1105.4 3.2 copy-start.3
  1112.4 60.8 %collective-permute-start.15 = (bf16[1024,2048]{1,0:T(8,128)(2,1)}, bf16[1024,2048]{1,0:T(8,128)(2,1)}, u32[]{:S(2)}, u32[]{:S(2)}) collective-permute-start(bf16[1024,2048]{1,0:T(8,128)(2,1)} %get-tuple-element.738), channel_id=1, source_target_pairs={{0,5},{1,0},{2,1},{3,2},{6,3},{7,6},{4,7},{5,4}} | collective-permute-start | bytes 12582920 | tf_op jit(solution)/shard_map/cond/branch_1_fun/ppermute | solution.py:285
  1112.4 60.8 %copy-start.27 = (s32[6144]{0:T(1024)S(1)}, s32[6144]{0:T(1024)}, u32[]{:S(2)}) copy-start(s32[6144]{0:T(1024)} %subtract_select_fusion) | copy-start | bytes 73732 | tf_op jit(solution)/shard_map/cond
  1112.4 60.8 %collective-permute-start.16 = (bf16[1024,2048]{1,0:T(8,128)(2,1)}, bf16[1024,2048]{1,0:T(8,128)(2,1)}, u32[]{:S(2)}, u32[]{:S(2)}) collective-permute-start(bf16[1024,2048]{1,0:T(8,128)(2,1)} %get-tuple-element.737), channel_id=1, source_target_pairs={{0,1},{1,2},{2,3},{3,6},{6,7},{7,4},{4,5},{5,0}} | collective-permute-start | bytes 12582920 | tf_op jit(solution)/shard_map/cond/branch_1_fun/ppermute | solution.py:286
  1179.4 10.1 copy-start.6
  1179.4 48.0 %collective-permute-start = (bf16[1024,2048]{1,0:T(8,128)(2,1)}, bf16[1024,2048]{1,0:T(8,128)(2,1)}, u32[]{:S(2)}, u32[]{:S(2)}) collective-permute-start(bf16[1024,2048]{1,0:T(8,128)(2,1)} %get-tuple-element.432), channel_id=1, source_target_pairs={{0,5},{1,0},{2,1},{3,2},{6,3},{7,6},{4,7},{5,4}} | collective-permute-start | bytes 12582920 | tf_op jit(solution)/shard_map/cond/branch_1_fun/cond/branch_2_fun/ppermute | solution.py:303
  1179.5 52.6 %collective-permute-start.1 = (bf16[1024,2048]{1,0:T(8,128)(2,1)}, bf16[1024,2048]{1,0:T(8,128)(2,1)}, u32[]{:S(2)}, u32[]{:S(2)}) collective-permute-start(bf16[1024,2048]{1,0:T(8,128)(2,1)} %get-tuple-element.432), channel_id=1, source_target_pairs={{0,1},{1,2},{2,3},{3,6},{6,7},{7,4},{4,5},{5,0}} | collective-permute-start | bytes 12582920 | tf_op jit(solution)/shard_map/cond/branch_1_fun/cond/branch_2_fun/ppermute | solution.py:304

commit v2 on v1

--- a/solution.py
+++ b/solution.py
@@ -17,6 +17,7 @@
 BQ = 512
 BK = 512
 HEAD_ROWS = 1024
+ROW_TILE = 512
 LEVELS = (1024, 1536, 2048, 3072)
 
 
@@ -215,6 +216,81 @@
     )(jnp.min(blocks, axis=1), jnp.max(blocks, axis=1), lo[:, None], q, kv, kv)
 
 
+def norm_block(x_ref, g_ref, rows):
+    x = x_ref[rows, :].astype(jnp.float32)
+    inv = lax.rsqrt(jnp.mean(x * x, axis=1, keepdims=True) + NORM_EPS)
+    return (x * inv * g_ref[...].astype(jnp.float32)).astype(jnp.bfloat16)
+
+
+def proj_kernel(x_ref, g_ref, cos_ref, sin_ref, w_ref, o_ref, *, turned):
+    h = norm_block(x_ref, g_ref, slice(None))
+    width = w_ref.shape[1]
+    for c in range(0, width, 256):
+        y = jnp.dot(h, w_ref[:, c:c + 256], preferred_element_type=jnp.float32)
+        for e in range(0, 256, 128):
+            part = y[:, e:e + 128]
+            if c + e < turned:
+                part = part * cos_ref[...] + pltpu.roll(part, 64, 1) * sin_ref[...]
+            o_ref[:, c + e:c + e + 128] = part.astype(jnp.bfloat16)
+
+
+def project(x, gain, cos2, sin2, w, turned):
+    n_rows, dim = x.shape
+    width = w.shape[1]
+    return pl.pallas_call(
+        functools.partial(proj_kernel, turned=turned),
+        grid=(n_rows // ROW_TILE,),
+        in_specs=[
+            pl.BlockSpec((ROW_TILE, dim), lambda i: (i, 0)),
+            pl.BlockSpec((1, dim), lambda i: (0, 0)),
+            pl.BlockSpec((ROW_TILE, 128), lambda i: (i, 0)),
+            pl.BlockSpec((ROW_TILE, 128), lambda i: (i, 0)),
+            pl.BlockSpec((dim, width), lambda i: (0, 0)),
+        ],
+        out_specs=pl.BlockSpec((ROW_TILE, width), lambda i: (i, 0)),
+        out_shape=jax.ShapeDtypeStruct((n_rows, width), jnp.bfloat16),
+        compiler_params=pltpu.CompilerParams(dimension_semantics=("arbitrary",)),
+        cost_estimate=pl.CostEstimate(flops=2 * n_rows * dim * width, bytes_accessed=2 * (n_rows * (dim + width) + dim * width), transcendentals=0),
+        name="project",
+    )(x, gain[None, :], cos2, sin2, w)
+
+
+def gate_up_kernel(z_ref, g_ref, wg_ref, wu_ref, o_ref, h_ref):
+    n_rows = z_ref.shape[0]
+
+    @pl.when(pl.program_id(0) == 0)
+    def _():
+        for r in range(0, n_rows, 256):
+            h_ref[r:r + 256, :] = norm_block(z_ref, g_ref, slice(r, r + 256))
+
+    for r in range(0, n_rows, ROW_TILE):
+        h = h_ref[r:r + ROW_TILE, :]
+        gate = jnp.dot(h, wg_ref[...], preferred_element_type=jnp.float32)
+        up = jnp.dot(h, wu_ref[...], preferred_element_type=jnp.float32)
+        o_ref[r:r + ROW_TILE, :] = (jax.nn.silu(gate) * up).astype(jnp.bfloat16)
+
+
+def gate_up(z, first, n_rows, gain, w_gate, w_up, tile=256):
+    dim = z.shape[1]
+    ff = w_gate.shape[1]
+    return pl.pallas_call(
+        gate_up_kernel,
+        grid=(ff // tile,),
+        in_specs=[
+            pl.BlockSpec((n_rows, dim), lambda j: (first // n_rows, 0)),
+            pl.BlockSpec((1, dim), lambda j: (0, 0)),
+            pl.BlockSpec((dim, tile), lambda j: (0, j)),
+            pl.BlockSpec((dim, tile), lambda j: (0, j)),
+        ],
+        out_specs=pl.BlockSpec((n_rows, tile), lambda j: (0, j)),
+        out_shape=jax.ShapeDtypeStruct((n_rows, ff), jnp.bfloat16),
+        scratch_shapes=[pltpu.VMEM((n_rows, dim), jnp.bfloat16)],
+        compiler_params=pltpu.CompilerParams(dimension_semantics=("arbitrary",)),
+        cost_estimate=pl.CostEstimate(flops=4 * n_rows * dim * ff, bytes_accessed=2 * (n_rows * (dim + ff) + 2 * dim * ff), transcendentals=n_rows * ff),
+        name="gate_up",
+    )(z, gain[None, :], w_gate, w_up)
+
+
 def ring_perm(n_dev, shift):
     order = ring_order(n_dev)
     return [(order[r], order[(r + shift) % n_dev]) for r in range(n_dev)]
@@ -234,58 +310,69 @@
     return totals, ends - totals, centre - excess
 
 
-def balanced_path(plan, hidden, g_attn, w_q, w_k, w_v, w_o, g_mlp, w_gate, w_up, w_down):
-    ext_idx, back_k, pos, n_left, n_right, bucket = plan
-    n_tok, model_dim = hidden.shape
-    n_cap = pos.shape[0]
+def balanced_path(plan, hidden, tok_perm, g_attn, w_q, w_k, w_v, w_o, g_mlp, w_gate, w_up, w_down):
+    ext_idx, from_at, every, off, total, n_left, n_right, bucket = plan
+    model_dim = hidden.shape[1]
+    n_cap = from_at.shape[0]
     n_dev = 8
     head = HEAD_ROWS
     up, down = ring_perm(n_dev, 1), ring_perm(n_dev, -1)
-    slot = jnp.arange(n_cap, dtype=jnp.int32)[:, None]
+    slot = jnp.arange(n_cap, dtype=jnp.int32)
     levels = LEVELS
+    n_kv, head_dim = w_k.shape[1:]
 
     def grab(idx):
         return hidden.at[idx].get(mode='promise_in_bounds')
 
     def exchange(cap):
         def run():
-            sent = grab(jnp.concatenate([ext_idx[n_cap - cap:n_cap], ext_idx[2 * n_cap:2 * n_cap + cap]]))
-            right = lax.ppermute(sent[:cap], 'sp', down)
-            left = lax.ppermute(sent[cap:], 'sp', up)
-            own = grab(ext_idx[n_cap:2 * n_cap])
-            pad = jnp.zeros((n_cap - cap, model_dim), hidden.dtype)
-            left = jnp.concatenate([left, pad], axis=0)
-            right = jnp.concatenate([pad, right], axis=0)
-
-            def pick(a, b):
-                return jnp.where(slot[a:b] < n_left, left[a:b], jnp.where(slot[a:b] >= n_cap - n_right, right[a:b], own[a:b]))
-
-            return jnp.concatenate([pick(n_cap - head, n_cap), pick(0, n_cap - head)], axis=0)
+            right = lax.ppermute(grab(ext_idx[n_cap - cap:n_cap]), 'sp', down)
+            left = lax.ppermute(grab(ext_idx[2 * n_cap:2 * n_cap + cap]), 'sp', up)
+            rows = row_major(grab(jnp.roll(ext_idx[n_cap:2 * n_cap], head)))
+            pos = every.reshape(-1).at[from_at].get(mode='promise_in_bounds')
+            cos_t, sin_t = rope_tables(jnp.roll(pos, head), head_dim)
+            cos2 = jnp.concatenate([cos_t, cos_t], axis=1)
+            sin2 = jnp.concatenate([-sin_t, sin_t], axis=1)
+            order = jnp.argsort(tok_perm)
+            back_k = jnp.where(order < total, order - off, 4 * n_cap).astype(jnp.int32)
+            w_kv = jnp.concatenate([w_k.reshape(model_dim, -1), w_v.reshape(model_dim, -1)], axis=1)
+
+            def merge(rows, stored, vals, keep):
+                size = vals.shape[0]
+                return rows.at[stored:stored + size].set(jnp.where(keep[:, None], vals, rows[stored:stored + size]))
+
+            step = jnp.arange(cap, dtype=jnp.int32)
+            keep_l, keep_r = step < n_left, step >= cap - n_right
+            cut = min(cap, n_cap - head)
+            rows = merge(rows, head, left[:cut], keep_l[:cut])
+            if cap > cut:
+                rows = merge(rows, 0, left[cut:], keep_l[cut:])
+            cut = max(cap - head, 0)
+            rows = merge(rows, 0, right[cut:], keep_r[cut:])
+            if cut:
+                rows = merge(rows, n_cap - cut, right[:cut], keep_r[:cut])
+            return rows, pos, cos2, sin2, back_k, w_q.reshape(model_dim, -1), w_kv
         return run
 
-    rows = row_major(lax.switch(bucket, [exchange(cap) for cap in levels]))
-    normed = row_major(rms_norm(rows, g_attn))
-    tables = lax.optimization_barrier(rope_tables(jnp.roll(pos, head), w_q.shape[2]))
-    n_kv, head_dim = w_k.shape[1:]
-    w_kv = jnp.concatenate([w_k.reshape(model_dim, -1), w_v.reshape(model_dim, -1)], axis=1)
-    kv_proj = row_major(jnp.dot(normed, w_kv, preferred_element_type=jnp.float32))
-    kv_width = n_kv * head_dim
-
-    def turn(proj):
-        return rope(proj.reshape(n_cap, -1, head_dim), tables).astype(jnp.bfloat16).reshape(n_cap, -1)
-
-    kv = row_major(jnp.concatenate([turn(kv_proj[:, :kv_width]), kv_proj[:, kv_width:].astype(jnp.bfloat16)], axis=1))
+    rows, pos, cos2, sin2, back_k, w_q2, w_kv = lax.switch(bucket, [exchange(cap) for cap in levels])
+    rows = row_major(rows)
+    kv = project(rows, g_attn, cos2, sin2, w_kv, n_kv * head_dim)
     kv_prev = lax.ppermute(kv, 'sp', up)
-    q_proj = row_major(jnp.dot(normed, w_q.reshape(model_dim, -1), preferred_element_type=jnp.float32))
-    q_rot = row_major(turn(q_proj))
+    q_rot = project(rows, g_attn, cos2, sin2, w_q2, w_q2.shape[1])
     kv = jnp.concatenate([kv_prev, kv], axis=0)
-    heads = flash(q_rot, kv, n_cap + slot[:, 0] - pos, head)
+    heads = flash(q_rot, kv, n_cap + slot - pos, head)
     resid_mid = row_major(attn_residual(rows, heads, w_o))
-    ends = row_major(mlp_residual(resid_mid[:2 * head], g_mlp, w_gate, w_up, w_down))
+
+    def mlp(first, n_rows):
+        z = resid_mid[first:first + n_rows]
+        acts = gate_up(resid_mid, first, n_rows, g_mlp, w_gate, w_up)
+        down_proj = jnp.dot(acts, w_down, preferred_element_type=jnp.float32).astype(jnp.bfloat16)
+        return row_major((z.astype(jnp.float32) + down_proj.astype(jnp.float32)).astype(jnp.bfloat16))
+
+    ends = mlp(0, 2 * head)
     from_next = lax.ppermute(ends[head:], 'sp', down)
     from_prev = lax.ppermute(ends[:head], 'sp', up)
-    resid_tail = lax.optimization_barrier((resid_mid[2 * head:], ends[:8]))[0]
-    middle = row_major(mlp_residual(resid_tail, g_mlp, w_gate, w_up, w_down))
+    middle = mlp(2 * head, n_cap - 2 * head)
 
     def give_back(cap):
         extra = max(cap - head, 0)
@@ -345,8 +432,6 @@
         ext_idx = lax.dynamic_slice(jnp.pad(tok_perm, (2 * n_cap, 2 * n_cap)), (n_cap + off,), (3 * n_cap,))
         n_left = jnp.maximum(-off, 0)
         n_right = jnp.maximum(off_next, 0)
-        order = jnp.argsort(tok_perm)
-        back_k = jnp.where(order < total, order - off, 4 * n_cap).astype(jnp.int32)
         reach = jnp.max(jnp.abs(offs))
         bucket = sum((reach > level).astype(jnp.int32) for level in LEVELS[:-1])
 
@@ -359,12 +444,10 @@
         in_run = jnp.arange(n_cap, dtype=jnp.int32)[:, None] - run_rel.reshape(1, -1)
         run_base = (jnp.arange(n_dev, dtype=jnp.int32)[None, :] * every.shape[1] + run_slot).reshape(1, -1)
         from_at = jnp.sum(jnp.where((in_run >= 0) & (in_run < runs.reshape(1, -1)), run_base + in_run, 0), axis=1)
-        pos = every.reshape(-1).at[from_at].get(mode='promise_in_bounds')
-
-        plan = (ext_idx, back_k, pos, n_left, n_right, bucket)
+        plan = (ext_idx, from_at, every, off, total, n_left, n_right, bucket)
 
         def ring(_):
-            return balanced_path(plan, hidden, *params)
+            return balanced_path(plan, hidden, tok_perm, *params)
 
         def general(_):
             return general_path(hidden, tok_perm, send_off, send_len, recv_off, recv_len, recv_doc, recv_pos, *params)

time: 1300 us -> 1110 us (0.85)
  the two profiles are of different devices: /device:TPU:3 before, /device:TPU:1 now
where the time goes in v2:
time: 1110 us
  Pallas kernels  511 us (46%)
  local copies, waits for them, and re-layouts  233 us (21%)
  matrix products  199 us (18%)
  starting transfers between devices  58.9 us (5%)
  other arithmetic  49.9 us (4%)
  loops' own time  34.2 us (3%)
    pallas_call x2, Pallas kernels, gate_up(): pl.pallas_call(gate_up_kernel, grid=(ff // tile,), in_specs=[pl.BlockSpec...  310 us
    dot_general x2, matrix products, mlp(): jnp.dot(acts, w_down, preferred_element_type=jnp.float32)  166 us
    pallas_call x1, Pallas kernels, flash(): pl.pallas_call(functools.partial(flash_kernel, base=n_rows, shift=shift,...  150 us
    gather x3, local copies, waits for them, and re-layouts, grab(): return hidden.at[idx].get(mode='promise_in_bounds')  84.1 us
    gather x1, local copies, waits for them, and re-layouts, run(): jnp.concatenate(parts, axis=0).at[place].get(mode='promise_in_bounds')  57.7 us
    ppermute x1, starting transfers between devices, run(): lax.ppermute(jnp.concatenate([middle[:n_mid], ends[:over]], axis=0), 'sp'...  52.8 us
    pallas_call x2, Pallas kernels, project(): pl.pallas_call(functools.partial(proj_kernel, turned=turned), grid=(n_row...  50.8 us
    cond x29, local copies, waits for them, and re-layouts  40.4 us
  transfers between devices with their start and end apart: 7, of which 1 were waited for; matrix products, arithmetic and copies ran while one was open for 19% of the time, Pallas kernels for 3%

profile of v2, /device:TPU:1, one launch (start us, length us, event | category | flops | bytes accessed | tf_op | source)
XLA Modules:
  0.0 1110.1 jit_solution(12821843195157592448)
XLA Ops:
  0.0 0.9 select_reduce_fusion.3
  0.9 1.3 fusion.103
  2.2 0.6 broadcast_in_dim.314
  2.9 0.8 concatenate.237
  3.7 11.0 all-gather.1
  15.2 0.7 fusion.104
  17.2 0.6 abs_reduce_fusion
  19.8 0.9 slice_reduce_fusion
  21.0 0.6 slice.498
  21.6 1.3 and_reduce_fusion
  24.1 1084.6 %conditional.3 = (bf16[6144,2048]{1,0:T(8,128)(2,1)}) conditional(s32[]{:T(128)} %convert_element_type.135, (s32[6144]{0:T(1024)}, s32[8]{0:T(128)}, s32[8]{0:T(128)}, s32[8]{0:T(128)}, s32[8]{0:T(128)}, /*index=5*/bf16[6144,2048]{1,0:T(8,128)(2,1)}, bf16[2048]{0:T(1024)(128)(2,1)}, bf16[2048,16,128]{2,1,0:T(8,128)(2,1)}, s32[3072]{0:T(1024)}, ...), branch_computations={%region_10.21_spmd, %region_21.37_spmd} | conditional | flops 553650946048 | bytes 2587438592 | solution.py:455
  27.9 1.2 dynamic_slice.29
  29.2 0.7 fusion.120
  30.5 1.3 subtract_subtract_fusion
  32.6 0.6 dynamic_slice.30
  33.2 1.3 broadcast_in_dim.306.g_ref
  34.5 0.8 pad_dynamic-slice_fusion
  35.8 177.9 %conditional = (bf16[3072,2048]{1,0:T(8,128)(2,1)}, s32[3072]{0:T(1024)}, s32[3072]{0:T(1024)S(1)}, f32[3072,128]{1,0:T(8,128)}, f32[3072,128]{1,0:T(8,128)}, /*...) conditional(s32[]{:T(128)} %clamp.0, (s32[9216]{0:T(1024)S(1)}, ...), branch_computations={%region_23.24_spmd, %region_25.26_spmd, %region_27.28_spmd, %regio... | conditional | flops 20198464 | bytes 357239776 | solution.py:357
  39.3 24.3 %gather_fusion.5 = bf16[1536,2048]{1,0:T(8,128)(2,1)} fusion(bf16[6144,2048]{1,0:T(8,128)(2,1)} %get-tuple-element.585, s32[2048]{0:T(1024)S(1)} %pad_clamp_fusion.1), kind=kCustom, calls=%fused_computation.10 | custom fusion | bytes 12589056 | tf_op jit(solution)/shard_map/cond/branch_1_fun/cond/branch_1_fun/gather | solution.py:325
  63.6 2.6 collective-permute-start.2
  66.3 24.2 %gather_fusion.6 = bf16[1536,2048]{1,0:T(8,128)(2,1)} fusion(bf16[6144,2048]{1,0:T(8,128)(2,1)} %get-tuple-element.585, s32[2048]{0:T(1024)S(1)} %pad_clamp_fusion), kind=kCustom, calls=%fused_computation.11 | custom fusion | bytes 12589056 | tf_op jit(solution)/shard_map/cond/branch_1_fun/cond/branch_1_fun/gather | solution.py:325
  90.6 30.5 %gather_fusion.7 = s32[3072]{0:T(1024)} fusion(s32[25600]{0:T(1024)S(1)} %reshape.1102, s32[3072]{0:T(1024)S(1)} %fusion.83), kind=kCustom, calls=%fused_computation.12 | custom fusion | bytes 36864 | tf_op jit(solution)/shard_map/cond/branch_1_fun/cond/branch_1_fun/gather | solution.py:332
  121.0 0.7 slice.578
  121.7 0.7 slice.577
  122.4 35.6 %gather_fusion.4 = bf16[3072,2048]{1,0:T(8,128)(2,1)} fusion(bf16[6144,2048]{1,0:T(8,128)(2,1)} %get-tuple-element.585, s32[3072]{0:T(1024)S(1)} %broadcast_clamp_fusion.6), kind=kCustom, calls=%fused_computation.9 | custom fusion | bytes 25178112 | tf_op jit(solution)/shard_map/cond/branch_1_fun/cond/branch_1_fun/gather | solution.py:325
  158.1 6.8 sort.70
  165.3 1.6 pad_maximum_fusion.5
  166.8 5.8 fusion.82
  172.6 2.5 pad_maximum_fusion.6
  175.2 8.8 fusion.79
  183.9 5.5 fusion.80
  189.4 4.1 fusion.81
  193.5 0.7 copy.221
  194.2 0.7 copy.222
  213.8 14.1 %project.3 = bf16[3072,512]{1,0:T(8,128)(2,1)} custom-call(bf16[3072,2048]{1,0:T(8,128)(2,1)} %get-tuple-element.663.x_ref, bf16[1,2048]{1,0:T(2,128)(2,1)} %broadcast_in_dim.306.g_ref, f32[3072,128]{1,0:T(8,128)} %get-tuple-element.666.cos_ref, f32[3072,128]{1,0:T(8,128)} %get-tuple-element.667.sin_ref, bf16[2048,512]{1,0:T(8,128)(2,1)} %get-tuple-element.669.w_ref), custom_call_target="tpu_custom_call" | custom-call | flops 6442450944 | bytes 17825792 | tf_op jit(solution)/shard_map/cond/branch_1_fun/project/pallas_call | solution.py:240
  227.9 1.7 collective-permute-start.14
  229.6 10.9 copy.126
  240.5 1.7 copy.86.lo_ref
  242.2 0.6 broadcast_in_dim.307.g_ref
  242.8 0.7 fusion.106
  243.5 1.2 subtract_select_fusion
  244.7 36.7 %project.2.q_ref = bf16[3072,2048]{1,0:T(8,128)(2,1)} custom-call(bf16[3072,2048]{1,0:T(8,128)(2,1)} %get-tuple-element.663.x_ref, bf16[1,2048]{1,0:T(2,128)(2,1)} %broadcast_in_dim.306.g_ref, f32[3072,128]{1,0:T(8,128)} %get-tuple-element.666.cos_ref, f32[3072,128]{1,0:T(8,128)} %get-tuple-element.667.sin_ref, bf16[2048,2048]{1,0:T(8,128)(2,1)} %bitcast.210), custom_call_target="tpu_custom_call" | custom-call | flops 25769803776 | bytes 33554432 | tf_op jit(solution)/shard_map/cond/branch_1_fun/project/pallas_call | solution.py:240
  281.4 4.9 pad_maximum_fusion.16.k_ref.v_ref
  286.3 149.7 %flash.1 = bf16[3072,2048]{1,0:T(8,128)(2,1)} custom-call(s32[6]{0:T(128)} %get-tuple-element.830.lomin_ref, s32[6]{0:T(128)} %get-tuple-element.829.lomax_ref, s32[3072,1]{1,0:T(8,128)} %copy.86.lo_ref, bf16[3072,2048]{1,0:T(8,128)(2,1)} %project.2.q_ref, bf16[6144,512]{1,0:T(8,128)(2,1)} %pad_maximum_fusion.16.k_ref.v_ref, ...), custom_call_target="tpu_custom_call" | custom-call | flops 80000000000 | bytes 40000000 | tf_op jit(solution)/shard_map/cond/branch_1_fun/flash/pallas_call | solution.py:193
  435.9 33.7 %add_convert_fusion.6.z_ref = bf16[3072,2048]{1,0:T(8,128)(2,1)} fusion(bf16[3072,2048]{1,0:T(8,128)(2,1)} %get-tuple-element.663.x_ref, bf16[3072,2048]{1,0:T(8,128)(2,1)} %flash.1, bf16[2048,2048]{1,0:T(8,128)(2,1)} %bitcast.260), kind=kOutput, calls=%fused_computation.271 | convolution fusion | flops 25801261056 | bytes 46137344 | tf_op jit(solution)/shard_map/cond/branch_1_fun/dot_general | solution.py:75
  469.6 107.0 %gate_up.3 = bf16[1024,11008]{1,0:T(8,128)(2,1)} custom-call(bf16[3072,2048]{1,0:T(8,128)(2,1)} %add_convert_fusion.6.z_ref, bf16[1,2048]{1,0:T(2,128)(2,1)} %broadcast_in_dim.307.g_ref, bf16[2048,11008]{1,0:T(8,128)(2,1)} %get-tuple-element.672.wg_ref, bf16[2048,11008]{1,0:T(8,128)(2,1)} %get-tuple-element.673.wu_ref), custom_call_target="tpu_custom_call" | custom-call | flops 92341796864 | bytes 116916224 | tf_op jit(solution)/shard_map/cond/branch_1_fun/gate_up/pallas_call | solution.py:276
  576.6 203.4 %gate_up.2 = bf16[2048,11008]{1,0:T(8,128)(2,1)} custom-call(bf16[3072,2048]{1,0:T(8,128)(2,1)} %add_convert_fusion.6.z_ref, bf16[1,2048]{1,0:T(2,128)(2,1)} %broadcast_in_dim.307.g_ref, bf16[2048,11008]{1,0:T(8,128)(2,1)} %get-tuple-element.672.wg_ref, bf16[2048,11008]{1,0:T(8,128)(2,1)} %get-tuple-element.673.wu_ref), custom_call_target="tpu_custom_call" | custom-call | flops 184683593728 | bytes 143654912 | tf_op jit(solution)/shard_map/cond/branch_1_fun/gate_up/pallas_call | solution.py:276
  780.1 106.2 %add_convert_fusion.7 = bf16[2048,2048]{1,0:T(8,128)(2,1)S(1)} fusion(bf16[3072,2048]{1,0:T(8,128)(2,1)} %add_convert_fusion.6.z_ref, bf16[2048,11008]{1,0:T(8,128)(2,1)} %gate_up.2, bf16[11008,2048]{1,0:T(8,128)(2,1)} %get-tuple-element.674), kind=kOutput, calls=%fused_computation.272 | convolution fusion | flops 92362768384 | bytes 106954752 | tf_op jit(solution)/shard_map/cond/branch_1_fun/dot_general | solution.py:369
  886.3 3.2 copy-done.6
  889.5 3.8 fusion.119
  893.3 1.7 collective-permute-start.16
  895.0 59.3 %add_convert_fusion.8 = bf16[1024,2048]{1,0:T(8,128)(2,1)} fusion(bf16[3072,2048]{1,0:T(8,128)(2,1)} %add_convert_fusion.6.z_ref, bf16[1024,11008]{1,0:T(8,128)(2,1)} %gate_up.3, bf16[11008,2048]{1,0:T(8,128)(2,1)} %get-tuple-element.674), kind=kOutput, calls=%fused_computation.274 | convolution fusion | flops 46181384192 | bytes 76021760 | tf_op jit(solution)/shard_map/cond/branch_1_fun/dot_general | solution.py:369
  954.4 6.7 collective-permute-done.16
  961.1 146.7 %conditional.1 = (bf16[6144,2048]{1,0:T(8,128)(2,1)}) conditional(s32[]{:T(128)} %clamp.0, (bf16[2048,2048]{1,0:T(8,128)(2,1)}, bf16[1024,2048]{1,0:T(8,128)(2,1)}, bf16[1024,2048]{1,0:T(8,128)(2,1)}, bf16[1024,2048]{1,0:T(8,128)(2,1)}, s32[6144]{0:T(1024)S(1)}) %tuple.260, (bf16[1024,2048]{1,0:T(8,128)(2,1)}, ...), branch_computations={%region_33.33_spmd, %region_34.34_spmd, %region_35.35_spmd, %regio... | conditional | flops 33751040 | bytes 255991904 | solution.py:400
  961.1 5.0 fusion.117
  966.1 52.8 %collective-permute-start.10 = (bf16[512,2048]{1,0:T(8,128)(2,1)}, bf16[512,2048]{1,0:T(8,128)(2,1)}, u32[]{:S(2)}, u32[]{:S(2)}) collective-permute-start(bf16[512,2048]{1,0:T(8,128)(2,1)} %get-tuple-element.916), channel_id=1, source_target_pairs={{0,5},{1,0},{2,1},{3,2},{6,3},{7,6},{4,7},{5,4}} | collective-permute-start | bytes 6291464 | tf_op jit(solution)/shard_map/cond/branch_1_fun/cond/branch_1_fun/ppermute | solution.py:390
  1018.9 8.3 constant_dynamic-update-slice_fusion.10
  1027.2 2.3 constant_dynamic-update-slice_fusion.9
  1029.5 4.9 constant_dynamic-update-slice_fusion.8
  1034.3 4.7 constant_dynamic-update-slice_fusion.7
  1039.1 3.2 constant_dynamic-update-slice_fusion.6
  1042.3 1.4 constant_dynamic-update-slice_fusion.5
  1043.7 0.6 broadcast_dynamic-update-slice_fusion.1
  1044.4 57.7 %gather_fusion.18 = bf16[6144,2048]{1,0:T(8,128)(2,1)} fusion(bf16[6160,2048]{1,0:T(8,128)(2,1)} %broadcast_dynamic-update-slice_fusion.1, s32[6144]{0:T(1024)S(1)} %fusion.99), kind=kCustom, calls=%fused_computation.22 | custom fusion | bytes 50356224 | tf_op jit(solution)/shard_map/cond/branch_1_fun/cond/branch_1_fun/gather | solution.py:397
  (72 shorter events, 2.1 us)
Async XLA Ops:
  14.7 9.3 copy-start.24
  15.9 4.8 copy-start.49
  63.6 111.5 %collective-permute-start.2 = (bf16[1536,2048]{1,0:T(8,128)(2,1)}, bf16[1536,2048]{1,0:T(8,128)(2,1)}, u32[]{:S(2)}, u32[]{:S(2)}) collective-permute-start(bf16[1536,2048]{1,0:T(8,128)(2,1)} %gather_fusion.5), channel_id=1, source_target_pairs={{0,1},{1,2},{2,3},{3,6},{6,7},{7,4},{4,5},{5,0}} | collective-permute-start | bytes 18874376 | tf_op jit(solution)/shard_map/cond/branch_1_fun/cond/branch_1_fun/ppermute | solution.py:330
  66.3 24.2 %copy-start.26 = (s32[8,3200]{1,0:T(8,128)S(1)}, s32[8,3200]{1,0:T(8,128)}, u32[]{:S(2)}) copy-start(s32[8,3200]{1,0:T(8,128)} %get-tuple-element.589) | copy-start | bytes 307204 | tf_op jit(solution)/shard_map/cond/branch_1_fun/cond
  90.5 93.5 %collective-permute-start.3 = (bf16[1536,2048]{1,0:T(8,128)(2,1)}, bf16[1536,2048]{1,0:T(8,128)(2,1)}, u32[]{:S(2)}, u32[]{:S(2)}) collective-permute-start(bf16[1536,2048]{1,0:T(8,128)(2,1)} %gather_fusion.6), channel_id=1, source_target_pairs={{0,5},{1,0},{2,1},{3,2},{6,3},{7,6},{4,7},{5,4}} | collective-permute-start | bytes 18874376 | tf_op jit(solution)/shard_map/cond/branch_1_fun/cond/branch_1_fun/ppermute | solution.py:329
  90.5 67.6 %copy-start.48 = (pred[1536]{0:T(1024)(128)(4,1)}, pred[1536]{0:T(1024)(128)(4,1)S(1)}, u32[]{:S(2)}) copy-start(pred[1536]{0:T(1024)(128)(4,1)S(1)} %iota_compare_fusion.4) | copy-start | bytes 4612 | tf_op jit(solution)/shard_map/cond/branch_1_fun/cond
  122.4 35.7 %copy-start.3 = (s32[6144]{0:T(1024)S(1)}, s32[6144]{0:T(1024)}, u32[]{:S(2)}) copy-start(s32[6144]{0:T(1024)} %get-tuple-element.594) | copy-start | bytes 73732 | tf_op jit(solution)/shard_map/cond/branch_1_fun/cond
  122.4 42.4 %copy-start.15 = (bf16[2048,2,128]{2,1,0:T(2,128)(2,1)S(1)}, bf16[2048,2,128]{2,1,0:T(2,128)(2,1)}, u32[]{:S(2)}) copy-start(bf16[2048,2,128]{2,1,0:T(2,128)(2,1)} %get-tuple-element.591) | copy-start | bytes 3145732 | tf_op jit(solution)/shard_map/cond/branch_1_fun/cond
  122.4 42.4 %copy-start.20 = (bf16[2048,2,128]{2,1,0:T(2,128)(2,1)S(1)}, bf16[2048,2,128]{2,1,0:T(2,128)(2,1)}, u32[]{:S(2)}) copy-start(bf16[2048,2,128]{2,1,0:T(2,128)(2,1)} %get-tuple-element.592) | copy-start | bytes 3145732 | tf_op jit(solution)/shard_map/cond/branch_1_fun/cond
  175.2 14.2 %slice-start.3 = ((pred[1536]{0:T(1024)(128)(4,1)}), pred[512]{0:T(512)(128)(4,1)S(1)}, s32[]{:S(2)}) async-start(pred[1536]{0:T(1024)(128)(4,1)} %copy-done.48), calls=%async_computation.5 | async-start | bytes 1024 | tf_op jit(solution)/shard_map/cond/branch_1_fun/cond/branch_1_fun/slice | solution.py:353
  227.9 14.3 %copy-start.39 = (bf16[2048]{0:T(1024)(128)(2,1)S(1)}, bf16[2048]{0:T(1024)(128)(2,1)}, u32[]{:S(2)}) copy-start(bf16[2048]{0:T(1024)(128)(2,1)} %get-tuple-element.671) | copy-start | bytes 12292 | tf_op jit(solution)/shard_map/cond
  227.9 53.5 %collective-permute-start.14 = (bf16[3072,512]{1,0:T(8,128)(2,1)}, bf16[3072,512]{1,0:T(8,128)(2,1)}, u32[]{:S(2)}, u32[]{:S(2)}) collective-permute-start(bf16[3072,512]{1,0:T(8,128)(2,1)} %project.3), channel_id=1, source_target_pairs={{0,1},{1,2},{2,3},{3,6},{6,7},{7,4},{4,5},{5,0}} | collective-permute-start | bytes 9437192 | tf_op jit(solution)/shard_map/cond/branch_1_fun/ppermute | solution.py:360
  244.7 36.7 %copy-start.23 = (bf16[3072,512]{1,0:T(8,128)(2,1)S(1)}, bf16[3072,512]{1,0:T(8,128)(2,1)}, u32[]{:S(2)}) copy-start(bf16[3072,512]{1,0:T(8,128)(2,1)} %project.3) | copy-start | bytes 9437188 | tf_op jit(solution)/shard_map/cond
  886.3 3.2 copy-start.6
  893.3 61.1 %collective-permute-start.15 = (bf16[1024,2048]{1,0:T(8,128)(2,1)}, bf16[1024,2048]{1,0:T(8,128)(2,1)}, u32[]{:S(2)}, u32[]{:S(2)}) collective-permute-start(bf16[1024,2048]{1,0:T(8,128)(2,1)} %get-tuple-element.922), channel_id=1, source_target_pairs={{0,5},{1,0},{2,1},{3,2},{6,3},{7,6},{4,7},{5,4}} | collective-permute-start | bytes 12582920 | tf_op jit(solution)/shard_map/cond/branch_1_fun/ppermute | solution.py:373
  893.3 67.8 %copy-start.32 = (s32[6144]{0:T(1024)S(1)}, s32[6144]{0:T(1024)}, u32[]{:S(2)}) copy-start(s32[6144]{0:T(1024)} %subtract_select_fusion) | copy-start | bytes 73732 | tf_op jit(solution)/shard_map/cond
  893.3 67.8 %collective-permute-start.16 = (bf16[1024,2048]{1,0:T(8,128)(2,1)}, bf16[1024,2048]{1,0:T(8,128)(2,1)}, u32[]{:S(2)}, u32[]{:S(2)}) collective-permute-start(bf16[1024,2048]{1,0:T(8,128)(2,1)} %get-tuple-element.921), channel_id=1, source_target_pairs={{0,1},{1,2},{2,3},{3,6},{6,7},{7,4},{4,5},{5,0}} | collective-permute-start | bytes 12582920 | tf_op jit(solution)/shard_map/cond/branch_1_fun/ppermute | solution.py:374
  961.1 66.1 %copy-start.8 = (bf16[1024,2048]{1,0:T(8,128)(2,1)S(1)}, bf16[1024,2048]{1,0:T(8,128)(2,1)}, u32[]{:S(2)}) copy-start(bf16[1024,2048]{1,0:T(8,128)(2,1)} %get-tuple-element.630) | copy-start | bytes 12582916 | tf_op jit(solution)/shard_map/cond/branch_1_fun/cond
  966.1 73.0 %collective-permute-start.10 = (bf16[512,2048]{1,0:T(8,128)(2,1)}, bf16[512,2048]{1,0:T(8,128)(2,1)}, u32[]{:S(2)}, u32[]{:S(2)}) collective-permute-start(bf16[512,2048]{1,0:T(8,128)(2,1)} %get-tuple-element.916), channel_id=1, source_target_pairs={{0,5},{1,0},{2,1},{3,2},{6,3},{7,6},{4,7},{5,4}} | collective-permute-start | bytes 6291464 | tf_op jit(solution)/shard_map/cond/branch_1_fun/cond/branch_1_fun/ppermute | solution.py:390
  1018.9 23.4 %collective-permute-start.11 = (bf16[512,2048]{1,0:T(8,128)(2,1)}, bf16[512,2048]{1,0:T(8,128)(2,1)S(1)}, u32[]{:S(2)}, u32[]{:S(2)}) collective-permute-start(bf16[512,2048]{1,0:T(8,128)(2,1)} %get-tuple-element.915), channel_id=1, source_target_pairs={{0,1},{1,2},{2,3},{3,6},{6,7},{7,4},{4,5},{5,0}} | collective-permute-start | bytes 6291464 | tf_op jit(solution)/shard_map/cond/branch_1_fun/cond/branch_1_fun/ppermute | solution.py:391
